TPU v7x, 128 devices: a whole 4x4x4 slice. The times are simulated.
128 devices in a mesh: band: 4 (over x_hi, core), grid: 32 (over z, x_lo, y).
Axes of the slice: x: 4 (x_hi: 2, x_lo: 2; x = x_hi * 2 + x_lo), y: 4, z: 4, core: 2. Of those that a mesh axis runs over, the one named last changes fastest.
Arguments:
- orbitals: float32 [8, 128, 128, 128], P('band', 'grid'), may hold values from -6 to 6
- occupation: float32 [8], P('band'), may hold values from 0.25 to 1
- g_list: int32 [524288], P('grid'), may hold values from 0 to 65535, as said below
- positions: float32 [3, 512], replicated, may hold values from 0 to 1
- species: int32 [512], replicated, may hold values from 0 to 3
- widths: float32 [4], replicated, may hold values from 0.3 to 2
Outputs:
- stress: float32 [3, 3], replicated
- atom_terms: float32 [512], replicated
Inputs may be any that keep to these rules, and one draw needn't show every extreme that they name: `g_list`: within each aligned block of 16384 entries the values are distinct and increasing.
All inputs are finite; a program needn't handle non-finite values.
Results may differ from a plain program's by a relative error of at most 0.00013.
Values sent between devices are 32-bit elements; how exact they have to be, the bound alone decides.
A program may use at most 64 MiB of HBM per device.

v0:
```python
import functools
import math

import jax
import jax.numpy as jnp
import numpy as np
from jax import lax
from jax.experimental import pallas as pl
from jax.experimental.pallas import tpu as pltpu
from jax.sharding import PartitionSpec as P

MESH = pl.DeviceIdType.MESH
N = 128
ATOMS = 512
BANDS = 8
TWO_PI = 2.0 * math.pi
F32 = jnp.float32
BF16 = jnp.bfloat16

WITHIN = ((0, 0), (1, 1), (2, 2), (3, 3), (0, 1), (2, 3), (0, 2), (1, 3), (0, 3), (1, 2))
CROSS = tuple((i, j) for i in range(4) for j in range(4, 8))
CHUNK_PLANES = (10, 8, 8, 10)
PLANES = 36


def table_parts():
    index = np.arange(N)
    angle = 2.0 * np.pi / N * ((index[:, None] * index[None, :]) % N)
    cos, sin = np.cos(angle), np.sin(angle)
    right = np.block([[cos, -sin], [sin, cos]])
    high = np.asarray(right, dtype=jnp.bfloat16)
    low = np.asarray(right - high.astype(np.float64), dtype=jnp.bfloat16)
    right_cat = np.concatenate([high, high, low], axis=0)
    left_cat = np.concatenate([high.T, high.T, low.T], axis=1)
    return right_cat, left_cat


def split(value):
    high = value.astype(BF16)
    low = (value - high.astype(F32)).astype(BF16)
    return high, low


def iota(shape, dim):
    return lax.broadcasted_iota(jnp.int32, shape, dim)


def fold(cell):
    return jnp.where(cell < N // 2, cell, cell - N)


def turns(value):
    return value - jnp.floor(value + 0.5)


def kernel(
    orbitals, occupation, g_list, positions, species, widths, right_table, left_table,
    out_atoms, out_stress,
    orb_v, list_v, neg_v, pos_v, spec_v, right_v, left_v,
    psi, y_buf, r_buf, z_re, z_im, zc_re, zc_im, x_re, x_im, col_x, col_z,
    red_src, red,
    load_sem, psi_send, psi_recv, neg_send, neg_recv, a2a_send, a2a_recv, red_send, red_recv,
):
    band = lax.axis_index("band")
    slab = lax.axis_index("grid")
    me = 4 * slab + band
    half = band // 2
    core = lax.rem(band, 2)
    pos_x = 2 * half + lax.rem(slab // 4, 2)
    pos_y = lax.rem(slab, 4)
    pos_z = slab // 8

    def target(step):
        mixed = lax.rem(step * 83, 128)
        to_core = lax.rem(core + mixed, 2)
        to_x = lax.rem(pos_x + mixed // 2, 4)
        to_y = lax.rem(pos_y + mixed // 8, 4)
        to_z = lax.rem(pos_z + mixed // 32, 4)
        to_band = 2 * (to_x // 2) + to_core
        to_slab = (2 * to_z + lax.rem(to_x, 2)) * 4 + to_y
        return to_band, to_slab

    barrier = pltpu.get_barrier_semaphore()

    def greet(step, carry):
        to_band, to_slab = target(step)
        pl.semaphore_signal(
            barrier, 1, device_id={"band": to_band, "grid": to_slab}, device_id_type=MESH
        )
        return carry

    loads = [
        pltpu.make_async_copy(src, dst, load_sem.at[k])
        for k, (src, dst) in enumerate(
            (
                (positions, pos_v),
                (species, spec_v),
                (orbitals, orb_v),
                (g_list, list_v),
                (right_table, right_v),
                (left_table, left_v),
            )
        )
    ]
    for load in loads:
        load.start()
    lax.fori_loop(1, N, greet, 0)

    loads[0].wait()
    loads[1].wait()
    kind = spec_v[...]
    width = jnp.zeros((1, ATOMS), F32)
    for s in range(4):
        width = jnp.where(kind == s, widths[s], width)
    spread = -0.5 * width * width
    low_row = iota((8, ATOMS), 0).astype(F32)
    high_row = iota((16, ATOMS), 0)
    high_row = jnp.where(high_row < 8, high_row, high_row - 16).astype(F32)
    for dim, re_ref, im_ref in ((0, x_re, x_im), (2, z_re, z_im)):
        where_at = pos_v[dim : dim + 1, :]
        low_turn = TWO_PI * turns(low_row * where_at)
        high_turn = TWO_PI * turns(high_row * turns(8.0 * where_at))
        low_cos, low_sin = jnp.cos(low_turn), jnp.sin(low_turn)
        high_cos, high_sin = jnp.cos(high_turn), jnp.sin(high_turn)
        for a in range(16):
            wave = (TWO_PI / N) * (low_row + float(8 * (a if a < 8 else a - 16)))
            form = jnp.exp(spread * (wave * wave))
            hc, hs = high_cos[a : a + 1, :], high_sin[a : a + 1, :]
            re_ref[8 * a : 8 * a + 8, :] = (hc * low_cos - hs * low_sin) * form
            im_ref[8 * a : 8 * a + 8, :] = (hc * low_sin + hs * low_cos) * form
    for table, cat in ((z_re, zc_re), (z_im, zc_im)):
        high, low = split(table[...])
        cat[0:N, :] = high
        cat[N : 2 * N, :] = high
        cat[2 * N : 3 * N, :] = low
    freq_y = fold(me)
    high_y = freq_y // 8
    low_y = freq_y - 8 * high_y
    at_y = pos_v[1:2, :]
    turn_y = TWO_PI * turns(
        low_y.astype(F32) * at_y + high_y.astype(F32) * turns(8.0 * at_y)
    )
    wave_y = (TWO_PI / N) * freq_y.astype(F32)
    form_y = jnp.exp(spread * (wave_y * wave_y))
    y_cos, y_sin = jnp.cos(turn_y) * form_y, jnp.sin(turn_y) * form_y

    loads[2].wait()
    for i in range(2):
        root = jnp.sqrt(jnp.full((N, N), occupation[i], F32))
        for plane in range(4):
            orb_v[i, plane] = orb_v[i, plane] * root
        psi[2 * band + i] = orb_v[i, band]

    pl.semaphore_wait(barrier, N - 1)

    mate = band + 1 - 2 * core
    trades = []
    for k, to_band in ((1, lax.rem(band + 2, 4)), (2, lax.rem(mate + 2, 4)), (0, mate)):
        trade = pltpu.make_async_remote_copy(
            orb_v.at[:, to_band],
            psi.at[pl.ds(2 * band, 2)],
            psi_send.at[k],
            psi_recv.at[k],
            device_id={"band": to_band, "grid": slab},
            device_id_type=MESH,
        )
        trade.start()
        trades.append(trade)
    loads[3].wait()
    neg_slab = jnp.where(band == 0, lax.rem(32 - slab, 32), 31 - slab)
    neg_copy = pltpu.make_async_remote_copy(
        list_v,
        neg_v,
        neg_send,
        neg_recv,
        device_id={"band": band, "grid": neg_slab},
        device_id_type=MESH,
    )

    @pl.when(neg_slab != slab)
    def _():
        neg_copy.start()

    @pl.when(neg_slab == slab)
    def _():
        neg_v[...] = list_v[...]

    loads[4].wait()
    loads[5].wait()

    def transform_yz(pairs, base, scales, first_plane, count):
        rows = []
        for q in range(count):
            parts = []
            for part in range(2):
                i, j = pairs[2 * q + part]
                rho = psi[base + i] * psi[base + j]
                scale = scales[2 * q + part]
                parts.append(rho if scale is None else rho * scale)
            rows.append(jnp.concatenate(parts, axis=1))
        high, low = split(jnp.concatenate(rows, axis=0))
        along_z = jnp.dot(
            jnp.concatenate([high, low, high], axis=1),
            right_v[...],
            preferred_element_type=F32,
        )
        columns = []
        for q in range(count):
            block = along_z[q * N : (q + 1) * N]
            columns.append(jnp.concatenate([block[:, :N], block[:, N:]], axis=0))
        high, low = split(jnp.concatenate(columns, axis=1))
        along_y = jnp.dot(
            left_v[...],
            jnp.concatenate([high, low, high], axis=0),
            preferred_element_type=F32,
        )
        for q in range(count):
            y_buf[first_plane + 2 * q] = along_y[:N, q * N : (q + 1) * N]
            y_buf[first_plane + 2 * q + 1] = along_y[N:, q * N : (q + 1) * N]

    def send(first_plane, planes, chunk):
        def one(step, carry):
            to_band, to_slab = target(step)
            pltpu.make_async_remote_copy(
                y_buf.at[pl.ds(first_plane, planes), 4 * to_slab + to_band, :],
                r_buf.at[pl.ds(first_plane, planes), me, :],
                a2a_send,
                a2a_recv.at[chunk],
                device_id={"band": to_band, "grid": to_slab},
                device_id_type=MESH,
            ).start()
            return carry

        lax.fori_loop(1, N, one, 0)

    root_two = math.sqrt(2.0)
    within_scale = [None if i == j else root_two for i, j in WITHIN]
    cross_scale = [root_two] * 8
    trades[2].wait_recv()
    transform_yz(WITHIN, 4 * half, within_scale, 26 * half, 5)
    send(26 * half, 10, 3 * half)
    trades[0].wait_recv()
    trades[1].wait_recv()
    transform_yz(CROSS[:8], 0, cross_scale, 10, 4)
    send(10, 8, 1)
    transform_yz(CROSS[8:], 0, cross_scale, 18, 4)
    send(18, 8, 2)
    transform_yz(WITHIN, 4 - 4 * half, within_scale, 26 - 26 * half, 5)
    send(26 - 26 * half, 10, 3 - 3 * half)

    for plane in range(PLANES):
        r_buf[plane, pl.ds(me, 1), :] = y_buf[plane, pl.ds(me, 1), :]

    @pl.when(neg_slab != slab)
    def _():
        neg_copy.wait_recv()

    def mask_of(list_ref, plane, negated):
        cells = list_ref[...]
        cell_x = lax.shift_right_logical(cells, 9)
        cell_z = cells & (N - 1)
        if negated:
            cell_x = (N - cell_x) & (N - 1)
            cell_z = (N - cell_z) & (N - 1)
        in_plane = (lax.shift_right_logical(cells, 7) & 3) == plane
        col_x[...] = jnp.where(in_plane, cell_x, -1)
        col_z[...] = cell_z
        row_index = iota((N, N), 0)

        def block(step, total):
            first = pl.multiple_of(step * 8, 8)
            block_x = col_x[pl.ds(first, 8), :]
            block_z = col_z[pl.ds(first, 8), :]
            hot_x = [(row_index == block_x[r : r + 1, :]).astype(F32).astype(BF16) for r in range(8)]
            hot_z = [(row_index == block_z[r : r + 1, :]).astype(F32).astype(BF16) for r in range(8)]
            return total + lax.dot_general(
                jnp.concatenate(hot_x, axis=1),
                jnp.concatenate(hot_z, axis=1),
                (((1,), (1,)), ((), ())),
                preferred_element_type=F32,
            )

        return lax.fori_loop(0, N // 8, block, jnp.zeros((N, N), F32))

    mask_here = mask_of(list_v, band, False)
    mask_neg = mask_of(neg_v, lax.rem(4 - band, 4), True)

    def power(first_plane, planes, chunk):
        arrived = r_buf.at[pl.ds(first_plane, planes), pl.ds(0, N - 1), :]
        pltpu.make_async_copy(arrived, arrived, a2a_recv.at[chunk]).wait()
        count = planes // 2
        columns = [
            jnp.concatenate(
                [r_buf[first_plane + 2 * q], r_buf[first_plane + 2 * q + 1]], axis=0
            )
            for q in range(count)
        ]
        high, low = split(jnp.concatenate(columns, axis=1))
        along_x = jnp.dot(
            left_v[...],
            jnp.concatenate([high, low, high], axis=0),
            preferred_element_type=F32,
        )
        total = None
        for q in range(count):
            real = along_x[:N, q * N : (q + 1) * N]
            imag = along_x[N:, q * N : (q + 1) * N]
            term = real * real + imag * imag
            total = term if total is None else total + term
        return total

    spectrum = power(10, 8, 1) + power(18, 8, 2)
    spectrum = spectrum + (power(0, 10, 0) + power(26, 10, 3))

    cell_x = iota((N, N), 0)
    cell_z = iota((N, N), 1)
    wave_x = (TWO_PI / N) * fold(cell_x).astype(F32)
    wave_z = (TWO_PI / N) * fold(cell_z).astype(F32)
    sign_x = jnp.where(cell_x == N // 2, -1.0, 1.0).astype(F32)
    sign_z = jnp.where(cell_z == N // 2, -1.0, 1.0).astype(F32)
    sign_y = jnp.where(me == N // 2, -1.0, 1.0).astype(F32)
    square = wave_x * wave_x + wave_y * wave_y + wave_z * wave_z
    nonzero = square > 0
    inverse = 1.0 / jnp.where(nonzero, square, 1.0)
    cells = float(N) ** 3
    scale = 0.5 * 4.0 * math.pi / (cells * cells * BANDS)
    weighted = jnp.where(nonzero, spectrum * scale * inverse, 0.0)
    here = weighted * mask_here
    there = weighted * mask_neg
    here_two = 2.0 * here * inverse
    there_two = 2.0 * there * inverse
    both_two = here_two + there_two
    total = here + there
    wave_xz = wave_x * wave_z
    terms = (
        both_two * (wave_x * wave_x) - total,
        wave_y * wave_x * (here_two + there_two * (sign_x * sign_y)),
        wave_xz * (here_two + there_two * (sign_x * sign_z)),
        both_two * (wave_y * wave_y) - total,
        wave_y * wave_z * (here_two + there_two * (sign_z * sign_y)),
        both_two * (wave_z * wave_z) - total,
    )
    lane = iota((1, N), 1)
    stress_row = jnp.zeros((1, N), F32)
    for term, lanes in zip(terms, ((0,), (1, 3), (2, 6), (4,), (5, 7), (8,))):
        value = jnp.sum(jnp.sum(term, axis=0, keepdims=True), axis=1, keepdims=True)
        for at in lanes:
            stress_row = jnp.where(lane == at, value, stress_row)

    def projected(rows, table):
        high, low = split(rows)
        return jnp.dot(
            jnp.concatenate([high, low, high], axis=1),
            table[...],
            preferred_element_type=F32,
        )

    proj_re = projected(jnp.concatenate([here, there], axis=0), zc_re)
    proj_im = projected(jnp.concatenate([here, there * sign_z], axis=0), zc_im)
    ex_re, ex_im = x_re[...], x_im[...]
    flip_im = jnp.where(iota((N, ATOMS), 0) == N // 2, -ex_im, ex_im)

    def along(re_part, im_part, table_im, sine):
        real = jnp.sum(ex_re * re_part - table_im * im_part, axis=0, keepdims=True)
        imag = jnp.sum(ex_re * im_part + table_im * re_part, axis=0, keepdims=True)
        return real * y_cos - imag * sine

    atoms = along(proj_re[:N], proj_im[:N], ex_im, y_sin)
    atoms = atoms + along(proj_re[N:], proj_im[N:], flip_im, y_sin * sign_y)
    for r in range(4):
        red_src[r : r + 1, :] = atoms[:, r * N : (r + 1) * N]
    red_src[4:5, :] = stress_row

    def share(step, carry):
        to_band, to_slab = target(step)
        pltpu.make_async_remote_copy(
            red_src.at[pl.ds(0, 5)],
            red.at[me, pl.ds(0, 5)],
            red_send,
            red_recv,
            device_id={"band": to_band, "grid": to_slab},
            device_id_type=MESH,
        ).start()
        return carry

    lax.fori_loop(1, N, share, 0)
    red[me, 0:5, :] = red_src[0:5, :]
    shared = red.at[pl.ds(0, N - 1), pl.ds(0, 5)]
    pltpu.make_async_copy(shared, shared, red_recv).wait()
    sums = jnp.sum(red[:, 0:5, :], axis=0)
    out_atoms[...] = sums[0:4]
    for r in range(3):
        row = sums[4:5, :]
        out_stress[r : r + 1, :] = (row if r == 0 else pltpu.roll(row, N - 3 * r, 1))[:, :3]

    for trade in trades:
        trade.wait_send()

    @pl.when(neg_slab != slab)
    def _():
        neg_copy.wait_send()

    sent = r_buf.at[:, pl.ds(0, N - 1), :]
    pltpu.make_async_copy(sent, sent, a2a_send).wait()
    pltpu.make_async_copy(shared, shared, red_send).wait()


def per_device(orbitals, occupation, g_list, positions, species, widths):
    right_table, left_table = table_parts()
    anywhere = pl.BlockSpec(memory_space=pl.ANY)
    scalars = pl.BlockSpec(memory_space=pltpu.SMEM)
    vector = pl.BlockSpec(memory_space=pltpu.VMEM)
    dma = pltpu.SemaphoreType.DMA
    atoms, stress = pl.pallas_call(
        kernel,
        out_shape=(
            jax.ShapeDtypeStruct((4, N), F32),
            jax.ShapeDtypeStruct((3, 3), F32),
        ),
        in_specs=[anywhere, scalars, anywhere, anywhere, anywhere, scalars, anywhere, anywhere],
        out_specs=(vector, vector),
        scratch_shapes=[
            pltpu.VMEM((2, 4, N, N), F32),
            pltpu.VMEM((N, N), jnp.int32),
            pltpu.VMEM((N, N), jnp.int32),
            pltpu.VMEM((3, ATOMS), F32),
            pltpu.VMEM((1, ATOMS), jnp.int32),
            pltpu.VMEM((6 * N, 2 * N), BF16),
            pltpu.VMEM((2 * N, 6 * N), BF16),
            pltpu.VMEM((BANDS, N, N), F32),
            pltpu.VMEM((PLANES, N, N), F32),
            pltpu.VMEM((PLANES, N, N), F32),
            pltpu.VMEM((N, ATOMS), F32),
            pltpu.VMEM((N, ATOMS), F32),
            pltpu.VMEM((3 * N, ATOMS), BF16),
            pltpu.VMEM((3 * N, ATOMS), BF16),
            pltpu.VMEM((N, ATOMS), F32),
            pltpu.VMEM((N, ATOMS), F32),
            pltpu.VMEM((N, N), jnp.int32),
            pltpu.VMEM((N, N), jnp.int32),
            pltpu.VMEM((8, N), F32),
            pltpu.VMEM((N, 8, N), F32),
            dma((6,)),
            dma((3,)),
            dma((3,)),
            dma,
            dma,
            dma,
            dma((4,)),
            dma,
            dma,
        ],
        compiler_params=pltpu.CompilerParams(
            collective_id=0, has_side_effects=True, vmem_limit_bytes=48 << 20
        ),
    )(
        orbitals,
        occupation,
        g_list.reshape(N, N),
        positions,
        species.reshape(1, ATOMS),
        widths,
        jnp.asarray(right_table),
        jnp.asarray(left_table),
    )
    return stress, atoms.reshape(ATOMS)


def solution(mesh):
    return jax.shard_map(
        per_device,
        mesh=mesh,
        in_specs=(P("band", "grid", None, None), P("band"), P("grid"), P(), P(), P()),
        out_specs=(P(), P()),
        check_vma=False,
    )
```

profile of v0, /device:TPU:1, one launch (start us, length us, event | category | flops | bytes accessed | tf_op | source)
XLA Modules:
  0.0 70.6 jit_solution(7952055523047882959)
XLA Ops:
  0.6 0.0 copy-start.5
  0.6 0.0 copy-start.6
  0.7 0.0 copy-start.7
  0.7 0.7 copy-done.5
  1.3 0.0 copy-done.6
  1.3 0.0 copy-done.7
  1.3 0.0 copy-start
  1.3 1.0 %copy-done = f32[2,4,128,128]{3,2,1,0:T(8,128)S(1)} copy-done((f32[2,4,128,128]{3,2,1,0:T(8,128)S(1)}, f32[2,4,128,128]{3,2,1,0:T(8,128)}, u32[]{:S(2)}) %copy-start) | copy-done | bytes 524312
  2.4 0.0 copy-start.1
  2.4 1.0 %copy-done.1 = bf16[256,768]{1,0:T(8,128)(2,1)S(1)} copy-done((bf16[256,768]{1,0:T(8,128)(2,1)S(1)}, bf16[256,768]{1,0:T(8,128)(2,1)}, u32[]{:S(2)}) %copy-start.1) | copy-done | bytes 393240
  3.4 0.0 copy-start.2
  3.4 1.0 %copy-done.2 = bf16[768,256]{1,0:T(8,128)(2,1)S(1)} copy-done((bf16[768,256]{1,0:T(8,128)(2,1)S(1)}, bf16[768,256]{1,0:T(8,128)(2,1)}, u32[]{:S(2)}) %copy-start.2) | copy-done | bytes 393240
  4.4 0.0 copy-start.3
  4.4 0.8 %copy-done.3 = s32[16384]{0:T(1024)S(1)} copy-done((s32[16384]{0:T(1024)S(1)}, s32[16384]{0:T(1024)}, u32[]{:S(2)}) %copy-start.3) | copy-done | bytes 65560
  5.2 0.0 copy-start.4
  5.2 0.7 copy-done.4
  5.9 63.5 %shard_map.95 = (f32[4,128]{1,0:T(4,128)S(1)}, f32[3,3]{1,0:T(4,128)S(1)}) custom-call(f32[2,4,128,128]{3,2,1,0:T(8,128)S(1)} %copy-done, f32[2]{0:T(128)S(1)} %copy-done.6, s32[128,128]{1,0:T(8,128)S(1)} %bitcast.3, f32[3,512]{1,0:T(4,128)S(1)} %copy-done.4, s32[1,512]{1,0:T(1,128)S(1)} %bitcast.4, f32[4]{0:T(128)S(1)} %copy-done.7, ...), custom_call_target="tpu_custom_call" | custom-call | tf_op jit(solution)/shard_map/pallas_call | solution.py:414
  69.4 0.6 copy.12
  70.0 0.6 copy.13
Async XLA Ops:
  0.6 0.7 copy-start.5
  0.6 0.7 copy-start.6
  0.7 0.7 copy-start.7
  1.3 1.0 %copy-start = (f32[2,4,128,128]{3,2,1,0:T(8,128)S(1)}, f32[2,4,128,128]{3,2,1,0:T(8,128)}, u32[]{:S(2)}) copy-start(f32[2,4,128,128]{3,2,1,0:T(8,128)} %orbitals.1) | copy-start | bytes 1572868
  2.4 1.0 %copy-start.1 = (bf16[256,768]{1,0:T(8,128)(2,1)S(1)}, bf16[256,768]{1,0:T(8,128)(2,1)}, u32[]{:S(2)}) copy-start(bf16[256,768]{1,0:T(8,128)(2,1)} %constant.5.clone.left_table) | copy-start | bytes 1179652
  3.4 1.0 %copy-start.2 = (bf16[768,256]{1,0:T(8,128)(2,1)S(1)}, bf16[768,256]{1,0:T(8,128)(2,1)}, u32[]{:S(2)}) copy-start(bf16[768,256]{1,0:T(8,128)(2,1)} %constant.4.clone.right_table) | copy-start | bytes 1179652
  4.4 0.8 %copy-start.3 = (s32[16384]{0:T(1024)S(1)}, s32[16384]{0:T(1024)}, u32[]{:S(2)}) copy-start(s32[16384]{0:T(1024)} %param.10) | copy-start | bytes 196612
  5.2 0.7 copy-start.4
where the time goes:
time: 71 us; the launch traced here: 70.6 us
  Pallas kernels  63.5 us (89%)
  local copies, waits for them, and re-layouts  6.39 us (9%)
    pallas_call x1, Pallas kernels, per_device(): pl.pallas_call(kernel, out_shape=(jax.ShapeDtypeStruct((4, N), F32), jax....  63.5 us
    unnamed x18, local copies, waits for them, and re-layouts  6.39 us

commit v1 on v0

--- a/solution.py
+++ b/solution.py
@@ -21,6 +21,15 @@
 CROSS = tuple((i, j) for i in range(4) for j in range(4, 8))
 CHUNK_PLANES = (10, 8, 8, 10)
 PLANES = 36
+
+
+def far_first():
+    steps = np.random.RandomState(1).permutation(np.arange(1, N))
+    moves = [(int(o) // 2 % 4, int(o) // 8 % 4, int(o) // 32, int(o) % 2) for o in steps]
+    return sorted(moves, key=lambda m: -sum(min(v, 4 - v) for v in m[:3]))
+
+
+MOVES = far_first()
 
 
 def table_parts():
@@ -58,7 +67,7 @@
     out_atoms, out_stress,
     orb_v, list_v, neg_v, pos_v, spec_v, right_v, left_v,
     psi, y_buf, r_buf, z_re, z_im, zc_re, zc_im, x_re, x_im, col_x, col_z,
-    red_src, red,
+    mask_v, red_src, red,
     load_sem, psi_send, psi_recv, neg_send, neg_recv, a2a_send, a2a_recv, red_send, red_recv,
 ):
     band = lax.axis_index("band")
@@ -70,24 +79,18 @@
     pos_y = lax.rem(slab, 4)
     pos_z = slab // 8
 
-    def target(step):
-        mixed = lax.rem(step * 83, 128)
-        to_core = lax.rem(core + mixed, 2)
-        to_x = lax.rem(pos_x + mixed // 2, 4)
-        to_y = lax.rem(pos_y + mixed // 8, 4)
-        to_z = lax.rem(pos_z + mixed // 32, 4)
-        to_band = 2 * (to_x // 2) + to_core
-        to_slab = (2 * to_z + lax.rem(to_x, 2)) * 4 + to_y
-        return to_band, to_slab
+    at_x = [lax.rem(pos_x + move, 4) for move in range(4)]
+    at_z = [8 * lax.rem(pos_z + move, 4) for move in range(4)]
+    at_y = [lax.rem(pos_y + move, 4) for move in range(4)]
+    at_core = [core, 1 - core]
+    bands = [[2 * (x // 2) + c for c in at_core] for x in at_x]
+    slabs = [[4 * lax.rem(x, 2) + y for y in at_y] for x in at_x]
+
+    def others():
+        for dx, dy, dz, dc in MOVES:
+            yield bands[dx][dc], slabs[dx][dy] + at_z[dz]
 
     barrier = pltpu.get_barrier_semaphore()
-
-    def greet(step, carry):
-        to_band, to_slab = target(step)
-        pl.semaphore_signal(
-            barrier, 1, device_id={"band": to_band, "grid": to_slab}, device_id_type=MESH
-        )
-        return carry
 
     loads = [
         pltpu.make_async_copy(src, dst, load_sem.at[k])
@@ -104,7 +107,10 @@
     ]
     for load in loads:
         load.start()
-    lax.fori_loop(1, N, greet, 0)
+    for to_band, to_slab in others():
+        pl.semaphore_signal(
+            barrier, 1, device_id={"band": to_band, "grid": to_slab}, device_id_type=MESH
+        )
 
     loads[0].wait()
     loads[1].wait()
@@ -151,6 +157,36 @@
             orb_v[i, plane] = orb_v[i, plane] * root
         psi[2 * band + i] = orb_v[i, band]
 
+    def mask_of(list_ref, plane, negated):
+        cells = list_ref[...]
+        cell_x = lax.shift_right_logical(cells, 9)
+        cell_z = cells & (N - 1)
+        if negated:
+            cell_x = (N - cell_x) & (N - 1)
+            cell_z = (N - cell_z) & (N - 1)
+        in_plane = (lax.shift_right_logical(cells, 7) & 3) == plane
+        col_x[...] = jnp.where(in_plane, cell_x, -1)
+        col_z[...] = cell_z
+        row_index = iota((N, N), 0)
+
+        def block(step, total):
+            first = pl.multiple_of(step * 8, 8)
+            block_x = col_x[pl.ds(first, 8), :]
+            block_z = col_z[pl.ds(first, 8), :]
+            hot_x = [(row_index == block_x[r : r + 1, :]).astype(F32).astype(BF16) for r in range(8)]
+            hot_z = [(row_index == block_z[r : r + 1, :]).astype(F32).astype(BF16) for r in range(8)]
+            return total + lax.dot_general(
+                jnp.concatenate(hot_x, axis=1),
+                jnp.concatenate(hot_z, axis=1),
+                (((1,), (1,)), ((), ())),
+                preferred_element_type=F32,
+            )
+
+        return lax.fori_loop(0, N // 8, block, jnp.zeros((N, N), F32))
+
+    loads[3].wait()
+    mask_v[...] = mask_of(list_v, band, False)
+
     pl.semaphore_wait(barrier, N - 1)
 
     mate = band + 1 - 2 * core
@@ -166,7 +202,6 @@
         )
         trade.start()
         trades.append(trade)
-    loads[3].wait()
     neg_slab = jnp.where(band == 0, lax.rem(32 - slab, 32), 31 - slab)
     neg_copy = pltpu.make_async_remote_copy(
         list_v,
@@ -219,8 +254,7 @@
             y_buf[first_plane + 2 * q + 1] = along_y[N:, q * N : (q + 1) * N]
 
     def send(first_plane, planes, chunk):
-        def one(step, carry):
-            to_band, to_slab = target(step)
+        for to_band, to_slab in others():
             pltpu.make_async_remote_copy(
                 y_buf.at[pl.ds(first_plane, planes), 4 * to_slab + to_band, :],
                 r_buf.at[pl.ds(first_plane, planes), me, :],
@@ -229,9 +263,6 @@
                 device_id={"band": to_band, "grid": to_slab},
                 device_id_type=MESH,
             ).start()
-            return carry
-
-        lax.fori_loop(1, N, one, 0)
 
     root_two = math.sqrt(2.0)
     within_scale = [None if i == j else root_two for i, j in WITHIN]
@@ -241,12 +272,12 @@
     send(26 * half, 10, 3 * half)
     trades[0].wait_recv()
     trades[1].wait_recv()
+    transform_yz(WITHIN, 4 - 4 * half, within_scale, 26 - 26 * half, 5)
+    send(26 - 26 * half, 10, 3 - 3 * half)
     transform_yz(CROSS[:8], 0, cross_scale, 10, 4)
     send(10, 8, 1)
     transform_yz(CROSS[8:], 0, cross_scale, 18, 4)
     send(18, 8, 2)
-    transform_yz(WITHIN, 4 - 4 * half, within_scale, 26 - 26 * half, 5)
-    send(26 - 26 * half, 10, 3 - 3 * half)
 
     for plane in range(PLANES):
         r_buf[plane, pl.ds(me, 1), :] = y_buf[plane, pl.ds(me, 1), :]
@@ -255,34 +286,6 @@
     def _():
         neg_copy.wait_recv()
 
-    def mask_of(list_ref, plane, negated):
-        cells = list_ref[...]
-        cell_x = lax.shift_right_logical(cells, 9)
-        cell_z = cells & (N - 1)
-        if negated:
-            cell_x = (N - cell_x) & (N - 1)
-            cell_z = (N - cell_z) & (N - 1)
-        in_plane = (lax.shift_right_logical(cells, 7) & 3) == plane
-        col_x[...] = jnp.where(in_plane, cell_x, -1)
-        col_z[...] = cell_z
-        row_index = iota((N, N), 0)
-
-        def block(step, total):
-            first = pl.multiple_of(step * 8, 8)
-            block_x = col_x[pl.ds(first, 8), :]
-            block_z = col_z[pl.ds(first, 8), :]
-            hot_x = [(row_index == block_x[r : r + 1, :]).astype(F32).astype(BF16) for r in range(8)]
-            hot_z = [(row_index == block_z[r : r + 1, :]).astype(F32).astype(BF16) for r in range(8)]
-            return total + lax.dot_general(
-                jnp.concatenate(hot_x, axis=1),
-                jnp.concatenate(hot_z, axis=1),
-                (((1,), (1,)), ((), ())),
-                preferred_element_type=F32,
-            )
-
-        return lax.fori_loop(0, N // 8, block, jnp.zeros((N, N), F32))
-
-    mask_here = mask_of(list_v, band, False)
     mask_neg = mask_of(neg_v, lax.rem(4 - band, 4), True)
 
     def power(first_plane, planes, chunk):
@@ -309,8 +312,9 @@
             total = term if total is None else total + term
         return total
 
-    spectrum = power(10, 8, 1) + power(18, 8, 2)
-    spectrum = spectrum + (power(0, 10, 0) + power(26, 10, 3))
+    spectrum = power(0, 10, 0) + power(26, 10, 3)
+    spectrum = spectrum + power(10, 8, 1)
+    spectrum = spectrum + power(18, 8, 2)
 
     cell_x = iota((N, N), 0)
     cell_z = iota((N, N), 1)
@@ -325,7 +329,7 @@
     cells = float(N) ** 3
     scale = 0.5 * 4.0 * math.pi / (cells * cells * BANDS)
     weighted = jnp.where(nonzero, spectrum * scale * inverse, 0.0)
-    here = weighted * mask_here
+    here = weighted * mask_v[...]
     there = weighted * mask_neg
     here_two = 2.0 * here * inverse
     there_two = 2.0 * there * inverse
@@ -371,8 +375,7 @@
         red_src[r : r + 1, :] = atoms[:, r * N : (r + 1) * N]
     red_src[4:5, :] = stress_row
 
-    def share(step, carry):
-        to_band, to_slab = target(step)
+    for to_band, to_slab in others():
         pltpu.make_async_remote_copy(
             red_src.at[pl.ds(0, 5)],
             red.at[me, pl.ds(0, 5)],
@@ -381,9 +384,6 @@
             device_id={"band": to_band, "grid": to_slab},
             device_id_type=MESH,
         ).start()
-        return carry
-
-    lax.fori_loop(1, N, share, 0)
     red[me, 0:5, :] = red_src[0:5, :]
     shared = red.at[pl.ds(0, N - 1), pl.ds(0, 5)]
     pltpu.make_async_copy(shared, shared, red_recv).wait()
@@ -407,7 +407,7 @@
 
 def per_device(orbitals, occupation, g_list, positions, species, widths):
     right_table, left_table = table_parts()
-    anywhere = pl.BlockSpec(memory_space=pl.ANY)
+    anywhere = pl.BlockSpec(memory_space=pltpu.HBM)
     scalars = pl.BlockSpec(memory_space=pltpu.SMEM)
     vector = pl.BlockSpec(memory_space=pltpu.VMEM)
     dma = pltpu.SemaphoreType.DMA
@@ -438,6 +438,7 @@
             pltpu.VMEM((N, ATOMS), F32),
             pltpu.VMEM((N, N), jnp.int32),
             pltpu.VMEM((N, N), jnp.int32),
+            pltpu.VMEM((N, N), F32),
             pltpu.VMEM((8, N), F32),
             pltpu.VMEM((N, 8, N), F32),
             dma((6,)),
@@ -451,7 +452,7 @@
             dma,
         ],
         compiler_params=pltpu.CompilerParams(
-            collective_id=0, has_side_effects=True, vmem_limit_bytes=48 << 20
+            collective_id=0, has_side_effects=True
         ),
     )(
         orbitals,

time: 71 us -> 59.3 us (0.84)
  Pallas kernels: 63.5 us -> 56.6 us
  local copies, waits for them, and re-layouts: 6.39 us -> 1.89 us
    pallas_call x1, Pallas kernels: 63.5 us -> 56.6 us  [per_device(): pl.pallas_call(kernel, out_shape=(jax.ShapeDtypeStruct((4, N), F32), jax....]
    unnamed x18 -> x6, local copies, waits for them, and re-layouts: 6.39 us -> 1.89 us
where the time goes in v1:
time: 59.3 us; the launch traced here: 59.1 us
  Pallas kernels  56.6 us (95%)
  local copies, waits for them, and re-layouts  1.89 us (3%)
  between operations  0.65 us (1%)
    pallas_call x1, Pallas kernels, per_device(): pl.pallas_call(kernel, out_shape=(jax.ShapeDtypeStruct((4, N), F32), jax....  56.6 us
    unnamed x6, local copies, waits for them, and re-layouts  1.89 us

profile of v1, /device:TPU:1, one launch (start us, length us, event | category | flops | bytes accessed | tf_op | source)
XLA Modules:
  0.0 59.1 jit_solution(10556897644797894462)
XLA Ops:
  0.6 56.6 %shard_map.95 = (f32[4,128]{1,0:T(4,128)}, f32[3,3]{1,0:T(4,128)}) custom-call(f32[2,4,128,128]{3,2,1,0:T(8,128)} %orbitals.1, f32[2]{0:T(128)} %occupation.1, s32[128,128]{1,0:T(8,128)} %bitcast.3, f32[3,512]{1,0:T(4,128)} %positions.1, s32[1,512]{1,0:T(1,128)} %bitcast.4, f32[4]{0:T(128)} %widths.1, bf16[768,256]{1,0:T(8,128)(2,1)} %constant.4.clone.right_table, ...), custom_call_target="tpu_custom_call" | custom-call | tf_op jit(solution)/shard_map/pallas_call | solution.py:414
  57.2 0.0 copy-start.1
  57.2 0.6 %copy-done.1 = f32[3,3]{1,0:T(4,128)S(1)} copy-done((f32[3,3]{1,0:T(4,128)S(1)}, f32[3,3]{1,0:T(4,128)}, u32[]{:S(2)}) %copy-start.1) | copy-done | bytes 60
  57.9 0.0 copy-start
  57.9 0.6 copy.12
  58.4 0.1 copy-done
  58.5 0.6 copy.13
Async XLA Ops:
  57.2 0.7 %copy-start.1 = (f32[3,3]{1,0:T(4,128)S(1)}, f32[3,3]{1,0:T(4,128)}, u32[]{:S(2)}) copy-start(f32[3,3]{1,0:T(4,128)} %get-tuple-element.8) | copy-start | bytes 112
  57.9 0.7 %copy-start = (f32[4,128]{1,0:T(4,128)S(1)}, f32[4,128]{1,0:T(4,128)}, u32[]{:S(2)}) copy-start(f32[4,128]{1,0:T(4,128)} %get-tuple-element.5) | copy-start | bytes 6148

commit v2 on v0

v2 whole, which is shorter than its diff:
```python
import functools
import math

import jax
import jax.numpy as jnp
import numpy as np
from jax import lax
from jax.experimental import pallas as pl
from jax.experimental.pallas import tpu as pltpu
from jax.sharding import PartitionSpec as P

MESH = pl.DeviceIdType.MESH
N = 128
ATOMS = 512
BANDS = 8
TWO_PI = 2.0 * math.pi
F32 = jnp.float32
BF16 = jnp.bfloat16

WITHIN = ((0, 0), (1, 1), (2, 2), (3, 3), (0, 1), (2, 3), (0, 2), (1, 3), (0, 3), (1, 2))
WITHIN_PARTS = 10
PARTS = 18


def far_first(moves):
    order = np.random.RandomState(1).permutation(len(moves))
    return sorted((moves[o] for o in order), key=lambda m: -sum(min(v, 4 - v) for v in m[:3]))


MOVES = far_first(
    [(x, y, z, c) for x in range(2) for y in range(4) for z in range(4) for c in range(2) if x + y + z + c]
)
GREETED = far_first(
    [
        (x, y, z, c)
        for x in range(4)
        for y in range(4)
        for z in range(4)
        for c in range(2)
        if x + y + z + c and (x != 2 or y + z == 0)
    ]
)


def table_parts():
    index = np.arange(N)
    angle = 2.0 * np.pi / N * ((index[:, None] * index[None, :]) % N)
    cos, sin = np.cos(angle), np.sin(angle)
    right = np.block([[cos, -sin], [sin, cos]])
    high = np.asarray(right, dtype=jnp.bfloat16)
    low = np.asarray(right - high.astype(np.float64), dtype=jnp.bfloat16)
    right_cat = np.concatenate([high, high, low], axis=0)
    left_cat = np.concatenate([high.T, high.T, low.T], axis=1)
    order = np.concatenate([index[0::2], index[1::2]])
    order = np.concatenate([order, N + order])
    high_x, low_x = high.T[:, order], low.T[:, order]
    cross_cat = np.concatenate([high_x, high_x, low_x], axis=1)
    return right_cat, left_cat, cross_cat


def split(value):
    high = value.astype(BF16)
    low = (value - high.astype(F32)).astype(BF16)
    return high, low


def iota(shape, dim):
    return lax.broadcasted_iota(jnp.int32, shape, dim)


def fold(cell):
    return jnp.where(cell < N // 2, cell, cell - N)


def turns(value):
    return value - jnp.floor(value + 0.5)


def kernel(
    orbitals, occupation, g_list, positions, species, widths, right_table, left_table, x_table,
    out_atoms, out_stress,
    orb_v, list_v, neg_v, pos_v, spec_v, right_v, left_v, tx_v,
    psi, y_buf, r_buf, z_re, z_im, zc_re, zc_im, x_re, x_im, col_x, col_z, masks,
    red_src, red_x, red_mid, red_yz,
    load_sem, mate_sem, cross_send, cross_recv, neg_sem, pass_sem, a2a_send, a2a_recv, red_sem,
):
    band = lax.axis_index("band")
    slab = lax.axis_index("grid")
    half = band // 2
    core = lax.rem(band, 2)
    low = lax.rem(slab // 4, 2)
    pos_x = 2 * half + low
    pos_y = lax.rem(slab, 4)
    pos_z = slab // 8
    owner = 2 * slab + core
    mate = band + 1 - 2 * core

    def device(to_band, to_slab):
        return dict(device_id={"band": to_band, "grid": to_slab}, device_id_type=MESH)

    at_x = [lax.rem(pos_x + move, 4) for move in range(4)]
    at_y = [lax.rem(pos_y + move, 4) for move in range(4)]
    at_z = [8 * lax.rem(pos_z + move, 4) for move in range(4)]
    at_core = [core, 1 - core]
    at_half = [half, 1 - half]
    lows = [[4 * at + y for y in at_y] for at in (low, 1 - low)]

    barrier = pltpu.get_barrier_semaphore()
    loads = [
        pltpu.make_async_copy(src, dst, load_sem.at[k])
        for k, (src, dst) in enumerate(
            (
                (positions, pos_v),
                (species, spec_v),
                (orbitals, orb_v),
                (g_list, list_v),
                (right_table, right_v),
                (left_table, left_v),
                (x_table, tx_v),
            )
        )
    ]
    for load in loads:
        load.start()
    greet_bands = [[2 * (x // 2) + c for c in at_core] for x in at_x]
    greet_slabs = [[4 * lax.rem(x, 2) + y for y in at_y] for x in at_x]
    for dx, dy, dz, dc in GREETED:
        pl.semaphore_signal(
            barrier, 1, **device(greet_bands[dx][dc], greet_slabs[dx][dy] + at_z[dz])
        )

    loads[0].wait()
    loads[1].wait()
    kind = spec_v[...]
    width = jnp.zeros((1, ATOMS), F32)
    for s in range(4):
        width = jnp.where(kind == s, widths[s], width)
    spread = -0.5 * width * width
    low_row = iota((8, ATOMS), 0).astype(F32)
    high_row = iota((16, ATOMS), 0)
    high_row = jnp.where(high_row < 8, high_row, high_row - 16).astype(F32)
    for dim, re_ref, im_ref in ((0, x_re, x_im), (2, z_re, z_im)):
        where_at = pos_v[dim : dim + 1, :]
        low_turn = TWO_PI * turns(low_row * where_at)
        high_turn = TWO_PI * turns(high_row * turns(8.0 * where_at))
        low_cos, low_sin = jnp.cos(low_turn), jnp.sin(low_turn)
        high_cos, high_sin = jnp.cos(high_turn), jnp.sin(high_turn)
        for a in range(16):
            wave = (TWO_PI / N) * (low_row + float(8 * (a if a < 8 else a - 16)))
            form = jnp.exp(spread * (wave * wave))
            hc, hs = high_cos[a : a + 1, :], high_sin[a : a + 1, :]
            re_ref[8 * a : 8 * a + 8, :] = (hc * low_cos - hs * low_sin) * form
            im_ref[8 * a : 8 * a + 8, :] = (hc * low_sin + hs * low_cos) * form
    for table, cat in ((z_re, zc_re), (z_im, zc_im)):
        high_part, low_part = split(table[...])
        cat[0:N, :] = high_part
        cat[N : 2 * N, :] = high_part
        cat[2 * N : 3 * N, :] = low_part
    y_waves = []
    at_turn = pos_v[1:2, :]
    for k in range(2):
        freq_y = fold(2 * owner + k)
        high_y = freq_y // 8
        low_y = freq_y - 8 * high_y
        turn_y = TWO_PI * turns(
            low_y.astype(F32) * at_turn + high_y.astype(F32) * turns(8.0 * at_turn)
        )
        wave_y = (TWO_PI / N) * freq_y.astype(F32)
        form_y = jnp.exp(spread * (wave_y * wave_y))
        y_waves.append((wave_y, jnp.cos(turn_y) * form_y, jnp.sin(turn_y) * form_y))

    loads[2].wait()
    for i in range(2):
        root = jnp.sqrt(jnp.full((N, N), occupation[i], F32))
        for plane in range(4):
            orb_v[i, plane] = orb_v[i, plane] * root
        for plane in range(2):
            psi[2 * band + i, plane] = orb_v[i, 2 * core + plane]

    pl.semaphore_wait(barrier, len(GREETED))

    loads[3].wait()
    neg_slab = jnp.where(core == 0, lax.rem(32 - slab, 32), 31 - slab)
    neg_copy = pltpu.make_async_remote_copy(
        list_v, neg_v.at[core], neg_sem.at[0], neg_sem.at[1], **device(band, neg_slab)
    )
    neg_pass = pltpu.make_async_remote_copy(
        neg_v.at[1], neg_v.at[1], pass_sem.at[0], pass_sem.at[1], **device(mate, slab)
    )

    @pl.when(neg_slab != slab)
    def _():
        neg_copy.start()

    @pl.when(neg_slab == slab)
    def _():
        neg_v[core] = list_v[...]

    def trade(to_band, to_core, send_sem, recv_sem):
        return pltpu.make_async_remote_copy(
            orb_v.at[:, pl.ds(2 * to_core, 2)],
            psi.at[pl.ds(2 * band, 2)],
            send_sem,
            recv_sem,
            **device(to_band, slab),
        )

    gives = jnp.logical_or(half == 0, core == low)
    gifts = [
        trade(2 * (1 - half) + to_core, to_core, cross_send.at[to_core], cross_recv.at[core])
        for to_core in range(2)
    ]

    @pl.when(gives)
    def _():
        for gift in gifts:
            gift.start()

    mate_trade = trade(mate, 1 - core, mate_sem.at[0], mate_sem.at[1])
    mate_trade.start()
    loads[4].wait()
    loads[5].wait()

    def transform_yz(pairs, base_i, base_j, scales, first_part, planes):
        blocks = [(q, plane) for plane in planes for q in range(len(pairs) // 2)]
        rows = []
        for q, plane in blocks:
            parts = []
            for part in range(2):
                i, j = pairs[2 * q + part]
                rho = psi[base_i + i, plane] * psi[base_j + j, plane]
                scale = scales[2 * q + part]
                parts.append(rho if scale is None else rho * scale)
            rows.append(jnp.concatenate(parts, axis=1))
        high_part, low_part = split(jnp.concatenate(rows, axis=0))
        along_z = jnp.dot(
            jnp.concatenate([high_part, low_part, high_part], axis=1),
            right_v[...],
            preferred_element_type=F32,
        )
        columns = []
        for n in range(len(blocks)):
            block = along_z[n * N : (n + 1) * N]
            columns.append(jnp.concatenate([block[:, :N], block[:, N:]], axis=0))
        high_part, low_part = split(jnp.concatenate(columns, axis=1))
        along_y = jnp.dot(
            left_v[...],
            jnp.concatenate([high_part, low_part, high_part], axis=0),
            preferred_element_type=F32,
        )
        for n, (q, plane) in enumerate(blocks):
            y_buf[first_part + 2 * q, plane] = along_y[:N, n * N : (n + 1) * N]
            y_buf[first_part + 2 * q + 1, plane] = along_y[N:, n * N : (n + 1) * N]

    def send(first_part, parts, first_plane, planes, chunk, halves):
        for dx, dy, dz, dc in MOVES:
            to_slab = lows[dx][dy] + at_z[dz]
            to_core = at_core[dc]
            to_row = pl.multiple_of(4 * to_slab + 2 * to_core, 2)
            my_row = pl.multiple_of(2 * owner, 2)
            where = (pl.ds(first_part, parts), pl.ds(first_plane, planes))
            pltpu.make_async_remote_copy(
                y_buf.at[(*where, pl.ds(to_row, 2))],
                r_buf.at[(*where, pl.ds(my_row, 2))],
                a2a_send,
                a2a_recv.at[chunk],
                **device(2 * halves[dx] + to_core, to_slab),
            ).start()

    root_two = math.sqrt(2.0)
    within_scale = [None if i == j else root_two for i, j in WITHIN]
    mate_trade.wait_recv()
    for plane in range(2):
        transform_yz(WITHIN, 4 * half, 4 * half, within_scale, 0, (plane,))
        send(0, WITHIN_PARTS, plane, 1, plane, [half, half])

    def mask_of(cells, chosen, columns, negated):
        cell_x = lax.shift_right_logical(cells, 9)
        cell_z = cells & (columns - 1)
        if negated:
            cell_x = (N - cell_x) & (N - 1)
            cell_z = (N - cell_z) & (N - 1)
        col_x[...] = jnp.where(chosen, cell_x, -1)
        col_z[...] = cell_z
        x_index = iota((N, N), 0)
        z_index = iota((columns, N), 0)

        def block(step, total):
            first = pl.multiple_of(step * 8, 8)
            block_x = col_x[pl.ds(first, 8), :]
            block_z = col_z[pl.ds(first, 8), :]
            hot_x = [(x_index == block_x[r : r + 1, :]).astype(F32).astype(BF16) for r in range(8)]
            hot_z = [(z_index == block_z[r : r + 1, :]).astype(F32).astype(BF16) for r in range(8)]
            return total + lax.dot_general(
                jnp.concatenate(hot_x, axis=1),
                jnp.concatenate(hot_z, axis=1),
                (((1,), (1,)), ((), ())),
                preferred_element_type=F32,
            )

        return lax.fori_loop(0, N // 8, block, jnp.zeros((N, columns), F32))

    own_cells = list_v[...]
    own_pair = (lax.shift_right_logical(own_cells, 8) & 1) == core
    own_masks = mask_of(own_cells, own_pair, 2 * N, False)
    masks[0] = own_masks[:, :N]
    masks[1] = own_masks[:, N:]

    cross_bytes = [trade(0, 0, cross_send.at[0], cross_recv.at[k]) for k in range(2)]

    @pl.when(jnp.logical_or(half == 1, low == 0))
    def _():
        cross_bytes[0].wait_recv()

    @pl.when(jnp.logical_or(half == 1, low == 1))
    def _():
        cross_bytes[1].wait_recv()

    cross_scale = [root_two] * 4
    kind_set = half + low - 2 * half * low
    for pair in range(2):
        pairs = [(2 * pair + i, j) for i in range(2) for j in range(2)]
        first_part = WITHIN_PARTS + 4 * pair
        transform_yz(pairs, 0, 4 + 2 * kind_set, cross_scale, first_part, (0, 1))
        send(first_part, 4, 0, 2, 2 + pair, at_half)

    @pl.when(neg_slab != slab)
    def _():
        neg_copy.wait_recv()

    @pl.when(core == 1)
    def _():
        neg_pass.start()

    own_row = pl.ds(pl.multiple_of(2 * owner, 2), 2)
    for part in range(PARTS):
        for plane in range(2):
            r_buf[part, plane, own_row, :] = y_buf[part, plane, own_row, :]

    neg_cells = neg_v[core]
    neg_plane = lax.shift_right_logical(neg_cells, 7) & 3
    masks[2] = mask_of(neg_cells, neg_plane == 2 * core, N, True)

    @pl.when(core == 0)
    def _():
        neg_pass.wait_recv()

    neg_cells = neg_v[1]
    neg_plane = lax.shift_right_logical(neg_cells, 7) & 3
    masks[3] = mask_of(neg_cells, neg_plane == 3 - 2 * core, N, True)
    loads[6].wait()

    def arrived(first_part, parts, first_plane, planes, chunk):
        there = r_buf.at[pl.ds(first_part, parts), pl.ds(first_plane, planes), pl.ds(0, N - 2)]
        pltpu.make_async_copy(there, there, a2a_recv.at[chunk]).wait()

    def power(first_part, count, totals):
        blocks = [(q, k) for q in range(count) for k in range(2)]
        columns = [
            jnp.concatenate(
                [
                    r_buf[first_part + 2 * q + part, plane, pl.ds(k, N // 2, stride=2), :]
                    for part in range(2)
                    for plane in range(2)
                ],
                axis=0,
            )
            for q, k in blocks
        ]
        high_part, low_part = split(jnp.concatenate(columns, axis=1))
        along_x = jnp.dot(
            tx_v[...],
            jnp.concatenate([high_part, low_part, high_part], axis=0),
            preferred_element_type=F32,
        )
        for n, (q, k) in enumerate(blocks):
            real = along_x[:N, n * N : (n + 1) * N]
            imag = along_x[N:, n * N : (n + 1) * N]
            term = real * real + imag * imag
            totals[k] = term if totals[k] is None else totals[k] + term
        return totals

    arrived(0, WITHIN_PARTS, 0, 1, 0)
    arrived(0, WITHIN_PARTS, 1, 1, 1)
    spectrum = power(0, 5, [None, None])
    arrived(WITHIN_PARTS, 4, 0, 2, 2)
    spectrum = power(WITHIN_PARTS, 2, spectrum)
    arrived(WITHIN_PARTS + 4, 4, 0, 2, 3)
    spectrum = power(WITHIN_PARTS + 4, 2, spectrum)

    cell_x = iota((N, N), 0)
    cell_z = iota((N, N), 1)
    wave_x = (TWO_PI / N) * fold(cell_x).astype(F32)
    wave_z = (TWO_PI / N) * fold(cell_z).astype(F32)
    sign_x = jnp.where(cell_x == N // 2, -1.0, 1.0).astype(F32)
    sign_z = jnp.where(cell_z == N // 2, -1.0, 1.0).astype(F32)
    cells = float(N) ** 3
    scale = 0.5 * 4.0 * math.pi / (cells * cells * BANDS)
    wave_xz = wave_x * wave_z
    stress_terms = None
    rows_re, rows_im = [], []
    signs_y = []
    for k in range(2):
        wave_y = y_waves[k][0]
        sign_y = jnp.where(2 * owner + k == N // 2, -1.0, 1.0).astype(F32)
        signs_y.append(sign_y)
        square = wave_x * wave_x + wave_y * wave_y + wave_z * wave_z
        nonzero = square > 0
        inverse = 1.0 / jnp.where(nonzero, square, 1.0)
        weighted = jnp.where(nonzero, spectrum[k] * scale * inverse, 0.0)
        here = weighted * masks[k]
        there = weighted * masks[2 + k]
        here_two = 2.0 * here * inverse
        there_two = 2.0 * there * inverse
        both_two = here_two + there_two
        total = here + there
        terms = (
            both_two * (wave_x * wave_x) - total,
            wave_y * wave_x * (here_two + there_two * (sign_x * sign_y)),
            wave_xz * (here_two + there_two * (sign_x * sign_z)),
            both_two * (wave_y * wave_y) - total,
            wave_y * wave_z * (here_two + there_two * (sign_z * sign_y)),
            both_two * (wave_z * wave_z) - total,
        )
        if stress_terms is None:
            stress_terms = terms
        else:
            stress_terms = [a + b for a, b in zip(stress_terms, terms)]
        rows_re += [here, there]
        rows_im += [here, there * sign_z]
    lane = iota((1, N), 1)
    stress_row = jnp.zeros((1, N), F32)
    for term, lanes in zip(stress_terms, ((0,), (1, 3), (2, 6), (4,), (5, 7), (8,))):
        value = jnp.sum(jnp.sum(term, axis=0, keepdims=True), axis=1, keepdims=True)
        for at in lanes:
            stress_row = jnp.where(lane == at, value, stress_row)

    def projected(rows, table):
        high_part, low_part = split(jnp.concatenate(rows, axis=0))
        return jnp.dot(
            jnp.concatenate([high_part, low_part, high_part], axis=1),
            table[...],
            preferred_element_type=F32,
        )

    proj_re = projected(rows_re, zc_re)
    proj_im = projected(rows_im, zc_im)
    ex_re, ex_im = x_re[...], x_im[...]
    flip_im = jnp.where(iota((N, ATOMS), 0) == N // 2, -ex_im, ex_im)
    atoms = jnp.zeros((1, ATOMS), F32)
    for n in range(4):
        re_part = proj_re[n * N : (n + 1) * N]
        im_part = proj_im[n * N : (n + 1) * N]
        k = n // 2
        table_im = flip_im if n % 2 else ex_im
        sine = y_waves[k][2] * signs_y[k] if n % 2 else y_waves[k][2]
        real = jnp.sum(ex_re * re_part - table_im * im_part, axis=0, keepdims=True)
        imag = jnp.sum(ex_re * im_part + table_im * re_part, axis=0, keepdims=True)
        atoms = atoms + (real * y_waves[k][1] - imag * sine)
    for r in range(4):
        red_src[r : r + 1, :] = atoms[:, r * N : (r + 1) * N]
    red_src[4:5, :] = stress_row

    def summed(source, parts, moves, slot, stage):
        used = source.at[pl.ds(0, 5)]
        for to_band, to_slab in moves:
            pltpu.make_async_remote_copy(
                used,
                parts.at[slot, pl.ds(0, 5)],
                red_sem.at[2 * stage],
                red_sem.at[2 * stage + 1],
                **device(to_band, to_slab),
            ).start()
        parts[slot, 0:5, :] = source[0:5, :]
        count = len(moves)
        shared = parts.at[pl.ds(0, count), pl.ds(0, 5)]
        pltpu.make_async_copy(shared, shared, red_sem.at[2 * stage + 1]).wait()
        return jnp.sum(parts[:, 0:5, :], axis=0), shared

    moves_x = [
        (greet_bands[dx][dc], greet_slabs[dx][0] + at_z[0])
        for dx in (2, 1, 3, 0)
        for dc in (1, 0)
        if dx + dc
    ]
    moves_yz = [
        (band, lows[0][dy] + at_z[dz])
        for dy, dz in sorted(
            ((dy, dz) for dy in range(4) for dz in range(4) if dy + dz),
            key=lambda m: -sum(min(v, 4 - v) for v in m),
        )
    ]
    middle, sent_x = summed(red_src, red_x, moves_x, 2 * pos_x + core, 0)
    red_mid[0:5, :] = middle
    sums, sent_yz = summed(red_mid, red_yz, moves_yz, 4 * pos_z + pos_y, 1)
    out_atoms[...] = sums[0:4]
    for r in range(3):
        row = sums[4:5, :]
        out_stress[r : r + 1, :] = (row if r == 0 else pltpu.roll(row, N - 3 * r, 1))[:, :3]

    mate_trade.wait_send()

    @pl.when(gives)
    def _():
        for gift in gifts:
            gift.wait_send()

    @pl.when(neg_slab != slab)
    def _():
        neg_copy.wait_send()

    @pl.when(core == 1)
    def _():
        neg_pass.wait_send()

    sent = r_buf.at[:, :, pl.ds(0, N - 2)]
    pltpu.make_async_copy(sent, sent, a2a_send).wait()
    pltpu.make_async_copy(sent_x, sent_x, red_sem.at[0]).wait()
    pltpu.make_async_copy(sent_yz, sent_yz, red_sem.at[2]).wait()


def per_device(orbitals, occupation, g_list, positions, species, widths):
    right_table, left_table, x_table = table_parts()
    anywhere = pl.BlockSpec(memory_space=pltpu.HBM)
    scalars = pl.BlockSpec(memory_space=pltpu.SMEM)
    vector = pl.BlockSpec(memory_space=pltpu.VMEM)
    dma = pltpu.SemaphoreType.DMA
    atoms, stress = pl.pallas_call(
        kernel,
        out_shape=(
            jax.ShapeDtypeStruct((4, N), F32),
            jax.ShapeDtypeStruct((3, 3), F32),
        ),
        in_specs=[anywhere, scalars, anywhere, anywhere, anywhere, scalars]
        + [anywhere] * 3,
        out_specs=(vector, vector),
        scratch_shapes=[
            pltpu.VMEM((2, 4, N, N), F32),
            pltpu.VMEM((N, N), jnp.int32),
            pltpu.VMEM((2, N, N), jnp.int32),
            pltpu.VMEM((3, ATOMS), F32),
            pltpu.VMEM((1, ATOMS), jnp.int32),
            pltpu.VMEM((6 * N, 2 * N), BF16),
            pltpu.VMEM((2 * N, 6 * N), BF16),
            pltpu.VMEM((2 * N, 6 * N), BF16),
            pltpu.VMEM((BANDS, 2, N, N), F32),
            pltpu.VMEM((PARTS, 2, N, N), F32),
            pltpu.VMEM((PARTS, 2, N, N), F32),
            pltpu.VMEM((N, ATOMS), F32),
            pltpu.VMEM((N, ATOMS), F32),
            pltpu.VMEM((3 * N, ATOMS), BF16),
            pltpu.VMEM((3 * N, ATOMS), BF16),
            pltpu.VMEM((N, ATOMS), F32),
            pltpu.VMEM((N, ATOMS), F32),
            pltpu.VMEM((N, N), jnp.int32),
            pltpu.VMEM((N, N), jnp.int32),
            pltpu.VMEM((4, N, N), F32),
            pltpu.VMEM((8, N), F32),
            pltpu.VMEM((8, 8, N), F32),
            pltpu.VMEM((8, N), F32),
            pltpu.VMEM((16, 8, N), F32),
            dma((7,)),
            dma((2,)),
            dma((2,)),
            dma((2,)),
            dma((2,)),
            dma((2,)),
            dma,
            dma((4,)),
            dma((4,)),
        ],
        compiler_params=pltpu.CompilerParams(collective_id=0, has_side_effects=True),
    )(
        orbitals,
        occupation,
        g_list.reshape(N, N),
        positions,
        species.reshape(1, ATOMS),
        widths,
        jnp.asarray(right_table),
        jnp.asarray(left_table),
        jnp.asarray(x_table),
    )
    return stress, atoms.reshape(ATOMS)


def solution(mesh):
    return jax.shard_map(
        per_device,
        mesh=mesh,
        in_specs=(P("band", "grid", None, None), P("band"), P("grid"), P(), P(), P()),
        out_specs=(P(), P()),
        check_vma=False,
    )
```

time: 71 us -> 54 us (0.76)
  Pallas kernels: 63.5 us -> 51.3 us
  local copies, waits for them, and re-layouts: 6.39 us -> 1.89 us
    pallas_call x1, Pallas kernels: 63.5 us -> 51.3 us  [per_device(): pl.pallas_call(kernel, out_shape=(jax.ShapeDtypeStruct((4, N), F32), jax....]
    unnamed x18 -> x6, local copies, waits for them, and re-layouts: 6.39 us -> 1.89 us
where the time goes in v2:
time: 54 us; the launch traced here: 53.8 us
  Pallas kernels  51.3 us (95%)
  local copies, waits for them, and re-layouts  1.89 us (4%)
  between operations  0.65 us (1%)
    pallas_call x1, Pallas kernels, per_device(): pl.pallas_call(kernel, out_shape=(jax.ShapeDtypeStruct((4, N), F32), jax....  51.3 us
    unnamed x6, local copies, waits for them, and re-layouts  1.89 us

profile of v2, /device:TPU:1, one launch (start us, length us, event | category | flops | bytes accessed | tf_op | source)
XLA Modules:
  0.0 53.8 jit_solution(2634540505311707131)
XLA Ops:
  0.6 51.3 %shard_map.104 = (f32[4,128]{1,0:T(4,128)}, f32[3,3]{1,0:T(4,128)}) custom-call(f32[2,4,128,128]{3,2,1,0:T(8,128)} %orbitals.1, f32[2]{0:T(128)} %occupation.1, s32[128,128]{1,0:T(8,128)} %bitcast.3, f32[3,512]{1,0:T(4,128)} %positions.1, s32[1,512]{1,0:T(1,128)} %bitcast.5, f32[4]{0:T(128)} %widths.1, bf16[768,256]{1,0:T(8,128)(2,1)} %constant.6.clone.right_table, ...), custom_call_target="tpu_custom_call" | custom-call | tf_op jit(solution)/shard_map/pallas_call | solution.py:528
  51.9 0.0 copy-start.1
  51.9 0.6 %copy-done.1 = f32[3,3]{1,0:T(4,128)S(1)} copy-done((f32[3,3]{1,0:T(4,128)S(1)}, f32[3,3]{1,0:T(4,128)}, u32[]{:S(2)}) %copy-start.1) | copy-done | bytes 60
  52.6 0.0 copy-start
  52.6 0.6 %copy.13 = f32[3,3]{1,0:T(4,128)} copy(f32[3,3]{1,0:T(4,128)S(1)} %copy-done.1) | data formatting | bytes 72
  53.1 0.1 copy-done
  53.2 0.6 %copy.14 = f32[512]{0:T(512)} copy(f32[512]{0:T(512)S(1)} %bitcast.4) | data formatting | bytes 4096
Async XLA Ops:
  51.9 0.7 %copy-start.1 = (f32[3,3]{1,0:T(4,128)S(1)}, f32[3,3]{1,0:T(4,128)}, u32[]{:S(2)}) copy-start(f32[3,3]{1,0:T(4,128)} %get-tuple-element.8) | copy-start | bytes 112
  52.6 0.7 %copy-start = (f32[4,128]{1,0:T(4,128)S(1)}, f32[4,128]{1,0:T(4,128)}, u32[]{:S(2)}) copy-start(f32[4,128]{1,0:T(4,128)} %get-tuple-element.5) | copy-start | bytes 6148

commit v3 on v2

--- a/solution.py
+++ b/solution.py
@@ -17,7 +17,7 @@
 F32 = jnp.float32
 BF16 = jnp.bfloat16
 
-WITHIN = ((0, 0), (1, 1), (2, 2), (3, 3), (0, 1), (2, 3), (0, 2), (1, 3), (0, 3), (1, 2))
+MIXED = (((0, 1), (2, 3)), ((0, 2), (1, 3)), ((0, 3), (1, 2)))
 WITHIN_PARTS = 10
 PARTS = 18
 
@@ -77,9 +77,9 @@
 
 
 def kernel(
-    orbitals, occupation, g_list, positions, species, widths, right_table, left_table, x_table,
+    orbitals, occupation_at, g_list, positions, species, widths_at, right_table, left_table, x_table,
     out_atoms, out_stress,
-    orb_v, list_v, neg_v, pos_v, spec_v, right_v, left_v, tx_v,
+    occupation, widths, orb_v, list_v, neg_v, pos_v, spec_v, right_v, left_v, tx_v,
     psi, y_buf, r_buf, z_re, z_im, zc_re, zc_im, x_re, x_im, col_x, col_z, masks,
     red_src, red_x, red_mid, red_yz,
     load_sem, mate_sem, cross_send, cross_recv, neg_sem, pass_sem, a2a_send, a2a_recv, red_sem,
@@ -117,11 +117,13 @@
                 (right_table, right_v),
                 (left_table, left_v),
                 (x_table, tx_v),
+                (occupation_at, occupation),
+                (widths_at, widths),
             )
         )
     ]
-    for load in loads:
-        load.start()
+    for k in (7, 2, 4, 5, 3, 0, 1, 8, 6):
+        loads[k].start()
     greet_bands = [[2 * (x // 2) + c for c in at_core] for x in at_x]
     greet_slabs = [[4 * lax.rem(x, 2) + y for y in at_y] for x in at_x]
     for dx, dy, dz, dc in GREETED:
@@ -129,8 +131,137 @@
             barrier, 1, **device(greet_bands[dx][dc], greet_slabs[dx][dy] + at_z[dz])
         )
 
+    loads[7].wait()
+    loads[2].wait()
+    for i in range(2):
+        root = jnp.sqrt(jnp.full((N, N), occupation[i], F32))
+        for plane in range(4):
+            orb_v[i, plane] = orb_v[i, plane] * root
+        for plane in range(2):
+            psi[2 * band + i, plane] = orb_v[i, 2 * core + plane]
+
+    def transform_yz(transforms, planes):
+        blocks = [(transform, plane) for plane in planes for transform in transforms]
+        rows = []
+        for (_, *pairs), plane in blocks:
+            parts = []
+            for i, j, scale in pairs:
+                rho = psi[i, plane] * psi[j, plane]
+                parts.append(rho if scale is None else rho * scale)
+            rows.append(jnp.concatenate(parts, axis=1))
+        high_part, low_part = split(jnp.concatenate(rows, axis=0))
+        along_z = jnp.dot(
+            jnp.concatenate([high_part, low_part, high_part], axis=1),
+            right_v[...],
+            preferred_element_type=F32,
+        )
+        columns = []
+        for n in range(len(blocks)):
+            block = along_z[n * N : (n + 1) * N]
+            columns.append(jnp.concatenate([block[:, :N], block[:, N:]], axis=0))
+        high_part, low_part = split(jnp.concatenate(columns, axis=1))
+        along_y = jnp.dot(
+            left_v[...],
+            jnp.concatenate([high_part, low_part, high_part], axis=0),
+            preferred_element_type=F32,
+        )
+        for n, ((part, *_), plane) in enumerate(blocks):
+            y_buf[part, plane] = along_y[:N, n * N : (n + 1) * N]
+            y_buf[part + 1, plane] = along_y[N:, n * N : (n + 1) * N]
+
+    def send(first_part, parts, first_plane, planes, chunk, halves, columns):
+        for dx, dy, dz, dc in MOVES:
+            if dx not in columns:
+                continue
+            to_slab = lows[dx][dy] + at_z[dz]
+            to_core = at_core[dc]
+            to_row = pl.multiple_of(4 * to_slab + 2 * to_core, 2)
+            my_row = pl.multiple_of(2 * owner, 2)
+            where = (pl.ds(first_part, parts), pl.ds(first_plane, planes))
+            pltpu.make_async_remote_copy(
+                y_buf.at[(*where, pl.ds(to_row, 2))],
+                r_buf.at[(*where, pl.ds(my_row, 2))],
+                a2a_send,
+                a2a_recv.at[chunk],
+                **device(2 * halves[dx] + to_core, to_slab),
+            ).start()
+
+    loads[4].wait()
+    loads[5].wait()
+    root_two = math.sqrt(2.0)
+    first = 4 * half
+    same_half = [half, half]
+
+    def within(part, band_at):
+        return (part, (band_at, band_at, None), (band_at + 1, band_at + 1, None))
+
+    transform_yz([within(8 * core, 2 * band)], (0, 1))
+
+    pl.semaphore_wait(barrier, len(GREETED))
+
+    loads[3].wait()
+    neg_slab = jnp.where(core == 0, lax.rem(32 - slab, 32), 31 - slab)
+    neg_copy = pltpu.make_async_remote_copy(
+        list_v, neg_v.at[core], neg_sem.at[0], neg_sem.at[1], **device(band, neg_slab)
+    )
+    neg_pass = pltpu.make_async_remote_copy(
+        neg_v.at[1], neg_v.at[1], pass_sem.at[0], pass_sem.at[1], **device(mate, slab)
+    )
+
+    @pl.when(neg_slab != slab)
+    def _():
+        neg_copy.start()
+
+    @pl.when(neg_slab == slab)
+    def _():
+        neg_v[core] = list_v[...]
+
+    def trade(to_band, to_core, send_sem, recv_sem):
+        return pltpu.make_async_remote_copy(
+            orb_v.at[:, pl.ds(2 * to_core, 2)],
+            psi.at[pl.ds(2 * band, 2)],
+            send_sem,
+            recv_sem,
+            **device(to_band, slab),
+        )
+
+    gives = jnp.logical_or(half == 0, core == low)
+    gives_late = jnp.logical_and(half == 0, core == 1)
+    gifts = [
+        trade(2 * (1 - half) + to_core, to_core, cross_send.at[to_core], cross_recv.at[core])
+        for to_core in range(2)
+    ]
+
+    @pl.when(jnp.logical_and(gives, jnp.logical_not(gives_late)))
+    def _():
+        for gift in gifts:
+            gift.start()
+
+    mate_trade = trade(mate, 1 - core, mate_sem.at[0], mate_sem.at[1])
+    mate_trade.start()
+    send(8 * core, 2, 0, 2, 0, same_half, (0, 1))
+
+    mate_trade.wait_recv()
+    rest = [within(8 - 8 * core, 2 * mate)]
+    for n, ((i, j), (k, m)) in enumerate(MIXED):
+        rest.append(
+            (2 + 2 * n, (first + i, first + j, root_two), (first + k, first + m, root_two))
+        )
+    for plane in range(2):
+        transform_yz(rest, (plane,))
+        send(2 - 2 * core, 8, plane, 1, 0, same_half, (0,))
+
+    @pl.when(gives_late)
+    def _():
+        for gift in gifts:
+            gift.start()
+
+    for plane in range(2):
+        send(2 - 2 * core, 8, plane, 1, 0, same_half, (1,))
+
     loads[0].wait()
     loads[1].wait()
+    loads[8].wait()
     kind = spec_v[...]
     width = jnp.zeros((1, ATOMS), F32)
     for s in range(4):
@@ -169,128 +300,30 @@
         form_y = jnp.exp(spread * (wave_y * wave_y))
         y_waves.append((wave_y, jnp.cos(turn_y) * form_y, jnp.sin(turn_y) * form_y))
 
-    loads[2].wait()
-    for i in range(2):
-        root = jnp.sqrt(jnp.full((N, N), occupation[i], F32))
-        for plane in range(4):
-            orb_v[i, plane] = orb_v[i, plane] * root
-        for plane in range(2):
-            psi[2 * band + i, plane] = orb_v[i, 2 * core + plane]
-
-    pl.semaphore_wait(barrier, len(GREETED))
-
-    loads[3].wait()
-    neg_slab = jnp.where(core == 0, lax.rem(32 - slab, 32), 31 - slab)
-    neg_copy = pltpu.make_async_remote_copy(
-        list_v, neg_v.at[core], neg_sem.at[0], neg_sem.at[1], **device(band, neg_slab)
-    )
-    neg_pass = pltpu.make_async_remote_copy(
-        neg_v.at[1], neg_v.at[1], pass_sem.at[0], pass_sem.at[1], **device(mate, slab)
-    )
-
-    @pl.when(neg_slab != slab)
-    def _():
-        neg_copy.start()
-
-    @pl.when(neg_slab == slab)
-    def _():
-        neg_v[core] = list_v[...]
-
-    def trade(to_band, to_core, send_sem, recv_sem):
-        return pltpu.make_async_remote_copy(
-            orb_v.at[:, pl.ds(2 * to_core, 2)],
-            psi.at[pl.ds(2 * band, 2)],
-            send_sem,
-            recv_sem,
-            **device(to_band, slab),
-        )
-
-    gives = jnp.logical_or(half == 0, core == low)
-    gifts = [
-        trade(2 * (1 - half) + to_core, to_core, cross_send.at[to_core], cross_recv.at[core])
-        for to_core in range(2)
-    ]
-
-    @pl.when(gives)
-    def _():
-        for gift in gifts:
-            gift.start()
-
-    mate_trade = trade(mate, 1 - core, mate_sem.at[0], mate_sem.at[1])
-    mate_trade.start()
-    loads[4].wait()
-    loads[5].wait()
-
-    def transform_yz(pairs, base_i, base_j, scales, first_part, planes):
-        blocks = [(q, plane) for plane in planes for q in range(len(pairs) // 2)]
-        rows = []
-        for q, plane in blocks:
-            parts = []
-            for part in range(2):
-                i, j = pairs[2 * q + part]
-                rho = psi[base_i + i, plane] * psi[base_j + j, plane]
-                scale = scales[2 * q + part]
-                parts.append(rho if scale is None else rho * scale)
-            rows.append(jnp.concatenate(parts, axis=1))
-        high_part, low_part = split(jnp.concatenate(rows, axis=0))
-        along_z = jnp.dot(
-            jnp.concatenate([high_part, low_part, high_part], axis=1),
-            right_v[...],
-            preferred_element_type=F32,
-        )
-        columns = []
-        for n in range(len(blocks)):
-            block = along_z[n * N : (n + 1) * N]
-            columns.append(jnp.concatenate([block[:, :N], block[:, N:]], axis=0))
-        high_part, low_part = split(jnp.concatenate(columns, axis=1))
-        along_y = jnp.dot(
-            left_v[...],
-            jnp.concatenate([high_part, low_part, high_part], axis=0),
-            preferred_element_type=F32,
-        )
-        for n, (q, plane) in enumerate(blocks):
-            y_buf[first_part + 2 * q, plane] = along_y[:N, n * N : (n + 1) * N]
-            y_buf[first_part + 2 * q + 1, plane] = along_y[N:, n * N : (n + 1) * N]
-
-    def send(first_part, parts, first_plane, planes, chunk, halves):
-        for dx, dy, dz, dc in MOVES:
-            to_slab = lows[dx][dy] + at_z[dz]
-            to_core = at_core[dc]
-            to_row = pl.multiple_of(4 * to_slab + 2 * to_core, 2)
-            my_row = pl.multiple_of(2 * owner, 2)
-            where = (pl.ds(first_part, parts), pl.ds(first_plane, planes))
-            pltpu.make_async_remote_copy(
-                y_buf.at[(*where, pl.ds(to_row, 2))],
-                r_buf.at[(*where, pl.ds(my_row, 2))],
-                a2a_send,
-                a2a_recv.at[chunk],
-                **device(2 * halves[dx] + to_core, to_slab),
-            ).start()
-
-    root_two = math.sqrt(2.0)
-    within_scale = [None if i == j else root_two for i, j in WITHIN]
-    mate_trade.wait_recv()
-    for plane in range(2):
-        transform_yz(WITHIN, 4 * half, 4 * half, within_scale, 0, (plane,))
-        send(0, WITHIN_PARTS, plane, 1, plane, [half, half])
-
     def mask_of(cells, chosen, columns, negated):
         cell_x = lax.shift_right_logical(cells, 9)
         cell_z = cells & (columns - 1)
         if negated:
             cell_x = (N - cell_x) & (N - 1)
             cell_z = (N - cell_z) & (N - 1)
-        col_x[...] = jnp.where(chosen, cell_x, -1)
-        col_z[...] = cell_z
-        x_index = iota((N, N), 0)
-        z_index = iota((columns, N), 0)
+        col_x[...] = jnp.where(chosen, cell_x, -1).astype(F32)
+        col_z[...] = cell_z.astype(F32)
+        x_index = iota((N, N), 0).astype(F32).astype(BF16)
+        z_index = iota((columns, N), 0).astype(F32).astype(BF16)
+        one, zero = jnp.ones((), BF16), jnp.zeros((), BF16)
+
+        def hot(index, block):
+            found = []
+            for r in range(8):
+                row = jnp.broadcast_to(block[r : r + 1, :], (16, N)).astype(BF16)
+                rows = jnp.concatenate([row] * (index.shape[0] // 16), axis=0)
+                found.append(jnp.where(index == rows, one, zero))
+            return found
 
         def block(step, total):
             first = pl.multiple_of(step * 8, 8)
-            block_x = col_x[pl.ds(first, 8), :]
-            block_z = col_z[pl.ds(first, 8), :]
-            hot_x = [(x_index == block_x[r : r + 1, :]).astype(F32).astype(BF16) for r in range(8)]
-            hot_z = [(z_index == block_z[r : r + 1, :]).astype(F32).astype(BF16) for r in range(8)]
+            hot_x = hot(x_index, col_x[pl.ds(first, 8), :])
+            hot_z = hot(z_index, col_z[pl.ds(first, 8), :])
             return total + lax.dot_general(
                 jnp.concatenate(hot_x, axis=1),
                 jnp.concatenate(hot_z, axis=1),
@@ -308,21 +341,26 @@
 
     cross_bytes = [trade(0, 0, cross_send.at[0], cross_recv.at[k]) for k in range(2)]
 
-    @pl.when(jnp.logical_or(half == 1, low == 0))
-    def _():
-        cross_bytes[0].wait_recv()
-
-    @pl.when(jnp.logical_or(half == 1, low == 1))
-    def _():
-        cross_bytes[1].wait_recv()
-
-    cross_scale = [root_two] * 4
     kind_set = half + low - 2 * half * low
+    other = 4 + 2 * kind_set
     for pair in range(2):
-        pairs = [(2 * pair + i, j) for i in range(2) for j in range(2)]
+        for sender in range(2):
+            from_both = jnp.logical_and(half == 1, sender == pair)
+            from_one = jnp.logical_and(half == 0, low == sender)
+
+            @pl.when(jnp.logical_or(from_both, from_one) if pair == 0 else from_both)
+            def _():
+                cross_bytes[sender].wait_recv()
+
         first_part = WITHIN_PARTS + 4 * pair
-        transform_yz(pairs, 0, 4 + 2 * kind_set, cross_scale, first_part, (0, 1))
-        send(first_part, 4, 0, 2, 2 + pair, at_half)
+        transform_yz(
+            [
+                (first_part + 2 * n, (i, other, root_two), (i, other + 1, root_two))
+                for n, i in enumerate((2 * pair, 2 * pair + 1))
+            ],
+            (0, 1),
+        )
+        send(first_part, 4, 0, 2, 1 + pair, at_half, (0, 1))
 
     @pl.when(neg_slab != slab)
     def _():
@@ -350,8 +388,8 @@
     masks[3] = mask_of(neg_cells, neg_plane == 3 - 2 * core, N, True)
     loads[6].wait()
 
-    def arrived(first_part, parts, first_plane, planes, chunk):
-        there = r_buf.at[pl.ds(first_part, parts), pl.ds(first_plane, planes), pl.ds(0, N - 2)]
+    def arrived(first_part, parts, chunk):
+        there = r_buf.at[pl.ds(first_part, parts), :, pl.ds(0, N - 2)]
         pltpu.make_async_copy(there, there, a2a_recv.at[chunk]).wait()
 
     def power(first_part, count, totals):
@@ -380,12 +418,11 @@
             totals[k] = term if totals[k] is None else totals[k] + term
         return totals
 
-    arrived(0, WITHIN_PARTS, 0, 1, 0)
-    arrived(0, WITHIN_PARTS, 1, 1, 1)
+    arrived(0, WITHIN_PARTS, 0)
     spectrum = power(0, 5, [None, None])
-    arrived(WITHIN_PARTS, 4, 0, 2, 2)
+    arrived(WITHIN_PARTS, 4, 1)
     spectrum = power(WITHIN_PARTS, 2, spectrum)
-    arrived(WITHIN_PARTS + 4, 4, 0, 2, 3)
+    arrived(WITHIN_PARTS + 4, 4, 2)
     spectrum = power(WITHIN_PARTS + 4, 2, spectrum)
 
     cell_x = iota((N, N), 0)
@@ -522,7 +559,6 @@
 def per_device(orbitals, occupation, g_list, positions, species, widths):
     right_table, left_table, x_table = table_parts()
     anywhere = pl.BlockSpec(memory_space=pltpu.HBM)
-    scalars = pl.BlockSpec(memory_space=pltpu.SMEM)
     vector = pl.BlockSpec(memory_space=pltpu.VMEM)
     dma = pltpu.SemaphoreType.DMA
     atoms, stress = pl.pallas_call(
@@ -531,10 +567,11 @@
             jax.ShapeDtypeStruct((4, N), F32),
             jax.ShapeDtypeStruct((3, 3), F32),
         ),
-        in_specs=[anywhere, scalars, anywhere, anywhere, anywhere, scalars]
-        + [anywhere] * 3,
+        in_specs=[anywhere] * 9,
         out_specs=(vector, vector),
         scratch_shapes=[
+            pltpu.SMEM((2,), F32),
+            pltpu.SMEM((4,), F32),
             pltpu.VMEM((2, 4, N, N), F32),
             pltpu.VMEM((N, N), jnp.int32),
             pltpu.VMEM((2, N, N), jnp.int32),
@@ -552,24 +589,26 @@
             pltpu.VMEM((3 * N, ATOMS), BF16),
             pltpu.VMEM((N, ATOMS), F32),
             pltpu.VMEM((N, ATOMS), F32),
-            pltpu.VMEM((N, N), jnp.int32),
-            pltpu.VMEM((N, N), jnp.int32),
+            pltpu.VMEM((N, N), F32),
+            pltpu.VMEM((N, N), F32),
             pltpu.VMEM((4, N, N), F32),
             pltpu.VMEM((8, N), F32),
             pltpu.VMEM((8, 8, N), F32),
             pltpu.VMEM((8, N), F32),
             pltpu.VMEM((16, 8, N), F32),
-            dma((7,)),
+            dma((9,)),
             dma((2,)),
             dma((2,)),
             dma((2,)),
             dma((2,)),
             dma((2,)),
             dma,
-            dma((4,)),
+            dma((3,)),
             dma((4,)),
         ],
-        compiler_params=pltpu.CompilerParams(collective_id=0, has_side_effects=True),
+        compiler_params=pltpu.CompilerParams(
+            collective_id=0, has_side_effects=True, vmem_limit_bytes=56538000
+        ),
     )(
         orbitals,
         occupation,

time: 54 us -> 52 us (0.963)
  Pallas kernels: 51.3 us -> 49.3 us
    pallas_call x1, Pallas kernels: 51.3 us -> 49.3 us  [per_device(): pl.pallas_call(kernel, out_shape=(jax.ShapeDtypeStruct((4, N), F32), jax....]
where the time goes in v3:
time: 52 us; the launch traced here: 51.7 us
  Pallas kernels  49.3 us (95%)
  local copies, waits for them, and re-layouts  1.81 us (3%)
  between operations  0.66 us (1%)
    pallas_call x1, Pallas kernels, per_device(): pl.pallas_call(kernel, out_shape=(jax.ShapeDtypeStruct((4, N), F32), jax....  49.3 us
    unnamed x6, local copies, waits for them, and re-layouts  1.81 us

profile of v3, /device:TPU:1, one launch (start us, length us, event | category | flops | bytes accessed | tf_op | source)
XLA Modules:
  0.0 51.7 jit_solution(495996700673114179)
XLA Ops:
  0.6 0.0 copy-start
  0.6 0.0 copy-start.1
  0.7 0.6 %copy-done = f32[2]{0:T(128)S(1)} copy-done((f32[2]{0:T(128)S(1)}, f32[2]{0:T(128)}, u32[]{:S(2)}) %copy-start) | copy-done | bytes 32
  1.3 0.0 copy-done.1
  1.3 49.3 %shard_map.104 = (f32[4,128]{1,0:T(4,128)S(1)}, f32[3,3]{1,0:T(4,128)S(1)}) custom-call(f32[2,4,128,128]{3,2,1,0:T(8,128)} %orbitals.1, f32[2]{0:T(128)S(1)} %copy-done, s32[128,128]{1,0:T(8,128)} %bitcast.4, f32[3,512]{1,0:T(4,128)} %positions.1, s32[1,512]{1,0:T(1,128)} %bitcast.5, f32[4]{0:T(128)S(1)} %copy-done.1, ...), custom_call_target="tpu_custom_call" | custom-call | tf_op jit(solution)/shard_map/pallas_call | solution.py:564
  50.6 0.6 %copy.13 = f32[3,3]{1,0:T(4,128)} copy(f32[3,3]{1,0:T(4,128)S(1)} %get-tuple-element.8) | data formatting | bytes 72
  51.2 0.6 %copy.14 = f32[512]{0:T(512)} copy(f32[512]{0:T(512)S(1)} %bitcast.3) | data formatting | bytes 4096
Async XLA Ops:
  0.6 0.7 %copy-start = (f32[2]{0:T(128)S(1)}, f32[2]{0:T(128)}, u32[]{:S(2)}) copy-start(f32[2]{0:T(128)} %occupation_at.1) | copy-start | bytes 28
  0.6 0.7 %copy-start.1 = (f32[4]{0:T(128)S(1)}, f32[4]{0:T(128)}, u32[]{:S(2)}) copy-start(f32[4]{0:T(128)} %widths_at.1) | copy-start | bytes 52

commit v4 on v3

--- a/solution.py
+++ b/solution.py
@@ -80,7 +80,7 @@
     orbitals, occupation_at, g_list, positions, species, widths_at, right_table, left_table, x_table,
     out_atoms, out_stress,
     occupation, widths, orb_v, list_v, neg_v, pos_v, spec_v, right_v, left_v, tx_v,
-    psi, y_buf, r_buf, z_re, z_im, zc_re, zc_im, x_re, x_im, col_x, col_z, masks,
+    psi, y_buf, r_buf, z_re, z_im, zc_re, zc_im, x_re, x_im, col_x, col_z, masks, coefs,
     red_src, red_x, red_mid, red_yz,
     load_sem, mate_sem, cross_send, cross_recv, neg_sem, pass_sem, a2a_send, a2a_recv, red_sem,
 ):
@@ -333,11 +333,16 @@
 
         return lax.fori_loop(0, N // 8, block, jnp.zeros((N, columns), F32))
 
-    own_cells = list_v[...]
-    own_pair = (lax.shift_right_logical(own_cells, 8) & 1) == core
-    own_masks = mask_of(own_cells, own_pair, 2 * N, False)
-    masks[0] = own_masks[:, :N]
-    masks[1] = own_masks[:, N:]
+    def own_mask():
+        own_cells = list_v[...]
+        own_pair = (lax.shift_right_logical(own_cells, 8) & 1) == core
+        own_masks = mask_of(own_cells, own_pair, 2 * N, False)
+        masks[0] = own_masks[:, :N]
+        masks[1] = own_masks[:, N:]
+
+    @pl.when(half == 1)
+    def _():
+        own_mask()
 
     cross_bytes = [trade(0, 0, cross_send.at[0], cross_recv.at[k]) for k in range(2)]
 
@@ -369,6 +374,10 @@
     @pl.when(core == 1)
     def _():
         neg_pass.start()
+
+    @pl.when(half == 0)
+    def _():
+        own_mask()
 
     own_row = pl.ds(pl.multiple_of(2 * owner, 2), 2)
     for part in range(PARTS):
@@ -418,13 +427,6 @@
             totals[k] = term if totals[k] is None else totals[k] + term
         return totals
 
-    arrived(0, WITHIN_PARTS, 0)
-    spectrum = power(0, 5, [None, None])
-    arrived(WITHIN_PARTS, 4, 1)
-    spectrum = power(WITHIN_PARTS, 2, spectrum)
-    arrived(WITHIN_PARTS + 4, 4, 2)
-    spectrum = power(WITHIN_PARTS + 4, 2, spectrum)
-
     cell_x = iota((N, N), 0)
     cell_z = iota((N, N), 1)
     wave_x = (TWO_PI / N) * fold(cell_x).astype(F32)
@@ -434,8 +436,6 @@
     cells = float(N) ** 3
     scale = 0.5 * 4.0 * math.pi / (cells * cells * BANDS)
     wave_xz = wave_x * wave_z
-    stress_terms = None
-    rows_re, rows_im = [], []
     signs_y = []
     for k in range(2):
         wave_y = y_waves[k][0]
@@ -444,27 +444,38 @@
         square = wave_x * wave_x + wave_y * wave_y + wave_z * wave_z
         nonzero = square > 0
         inverse = 1.0 / jnp.where(nonzero, square, 1.0)
-        weighted = jnp.where(nonzero, spectrum[k] * scale * inverse, 0.0)
-        here = weighted * masks[k]
-        there = weighted * masks[2 + k]
+        weight = jnp.where(nonzero, scale * inverse, 0.0)
+        here = weight * masks[k]
+        there = weight * masks[2 + k]
         here_two = 2.0 * here * inverse
         there_two = 2.0 * there * inverse
         both_two = here_two + there_two
         total = here + there
-        terms = (
-            both_two * (wave_x * wave_x) - total,
-            wave_y * wave_x * (here_two + there_two * (sign_x * sign_y)),
-            wave_xz * (here_two + there_two * (sign_x * sign_z)),
-            both_two * (wave_y * wave_y) - total,
-            wave_y * wave_z * (here_two + there_two * (sign_z * sign_y)),
-            both_two * (wave_z * wave_z) - total,
-        )
-        if stress_terms is None:
-            stress_terms = terms
-        else:
-            stress_terms = [a + b for a, b in zip(stress_terms, terms)]
+        coefs[k, 0] = here
+        coefs[k, 1] = there
+        coefs[k, 2] = both_two * (wave_x * wave_x) - total
+        coefs[k, 3] = wave_y * wave_x * (here_two + there_two * (sign_x * sign_y))
+        coefs[k, 4] = wave_xz * (here_two + there_two * (sign_x * sign_z))
+        coefs[k, 5] = both_two * (wave_y * wave_y) - total
+        coefs[k, 6] = wave_y * wave_z * (here_two + there_two * (sign_z * sign_y))
+        coefs[k, 7] = both_two * (wave_z * wave_z) - total
+
+    arrived(0, WITHIN_PARTS, 0)
+    spectrum = power(0, 5, [None, None])
+    arrived(WITHIN_PARTS, 4, 1)
+    spectrum = power(WITHIN_PARTS, 2, spectrum)
+    arrived(WITHIN_PARTS + 4, 4, 2)
+    spectrum = power(WITHIN_PARTS + 4, 2, spectrum)
+
+    rows_re, rows_im = [], []
+    for k in range(2):
+        here = spectrum[k] * coefs[k, 0]
+        there = spectrum[k] * coefs[k, 1]
         rows_re += [here, there]
         rows_im += [here, there * sign_z]
+    stress_terms = [
+        spectrum[0] * coefs[0, 2 + n] + spectrum[1] * coefs[1, 2 + n] for n in range(6)
+    ]
     lane = iota((1, N), 1)
     stress_row = jnp.zeros((1, N), F32)
     for term, lanes in zip(stress_terms, ((0,), (1, 3), (2, 6), (4,), (5, 7), (8,))):
@@ -592,6 +603,7 @@
             pltpu.VMEM((N, N), F32),
             pltpu.VMEM((N, N), F32),
             pltpu.VMEM((4, N, N), F32),
+            pltpu.VMEM((2, 8, N, N), F32),
             pltpu.VMEM((8, N), F32),
             pltpu.VMEM((8, 8, N), F32),
             pltpu.VMEM((8, N), F32),

time: 52 us -> 51.5 us (level)
  Pallas kernels: 49.3 us -> 48.7 us
    pallas_call x1, Pallas kernels: 49.3 us -> 48.7 us  [per_device(): pl.pallas_call(kernel, out_shape=(jax.ShapeDtypeStruct((4, N), F32), jax....]
where the time goes in v4:
time: 51.5 us; the launch traced here: 51.1 us
  Pallas kernels  48.7 us (95%)
  local copies, waits for them, and re-layouts  1.81 us (4%)
  between operations  0.66 us (1%)
    pallas_call x1, Pallas kernels, per_device(): pl.pallas_call(kernel, out_shape=(jax.ShapeDtypeStruct((4, N), F32), jax....  48.7 us
    unnamed x6, local copies, waits for them, and re-layouts  1.81 us

profile of v4, /device:TPU:1, one launch (start us, length us, event | category | flops | bytes accessed | tf_op | source)
XLA Modules:
  0.0 51.1 jit_solution(1550464466546360076)
XLA Ops:
  0.6 0.0 copy-start
  0.6 0.0 copy-start.1
  0.7 0.6 %copy-done = f32[2]{0:T(128)S(1)} copy-done((f32[2]{0:T(128)S(1)}, f32[2]{0:T(128)}, u32[]{:S(2)}) %copy-start) | copy-done | bytes 32
  1.3 0.0 copy-done.1
  1.3 48.7 %shard_map.104 = (f32[4,128]{1,0:T(4,128)S(1)}, f32[3,3]{1,0:T(4,128)S(1)}) custom-call(f32[2,4,128,128]{3,2,1,0:T(8,128)} %orbitals.1, f32[2]{0:T(128)S(1)} %copy-done, s32[128,128]{1,0:T(8,128)} %bitcast.4, f32[3,512]{1,0:T(4,128)} %positions.1, s32[1,512]{1,0:T(1,128)} %bitcast.5, f32[4]{0:T(128)S(1)} %copy-done.1, ...), custom_call_target="tpu_custom_call" | custom-call | tf_op jit(solution)/shard_map/pallas_call | solution.py:575
  50.0 0.6 %copy.13 = f32[3,3]{1,0:T(4,128)} copy(f32[3,3]{1,0:T(4,128)S(1)} %get-tuple-element.8) | data formatting | bytes 72
  50.5 0.6 %copy.14 = f32[512]{0:T(512)} copy(f32[512]{0:T(512)S(1)} %bitcast.3) | data formatting | bytes 4096
Async XLA Ops:
  0.6 0.7 %copy-start = (f32[2]{0:T(128)S(1)}, f32[2]{0:T(128)}, u32[]{:S(2)}) copy-start(f32[2]{0:T(128)} %occupation_at.1) | copy-start | bytes 28
  0.6 0.7 %copy-start.1 = (f32[4]{0:T(128)S(1)}, f32[4]{0:T(128)}, u32[]{:S(2)}) copy-start(f32[4]{0:T(128)} %widths_at.1) | copy-start | bytes 52

commit v5 on v4

--- a/solution.py
+++ b/solution.py
@@ -239,7 +239,7 @@
 
     mate_trade = trade(mate, 1 - core, mate_sem.at[0], mate_sem.at[1])
     mate_trade.start()
-    send(8 * core, 2, 0, 2, 0, same_half, (0, 1))
+    send(8 * core, 2, 0, 2, 0, same_half, (0,))
 
     mate_trade.wait_recv()
     rest = [within(8 - 8 * core, 2 * mate)]
@@ -256,6 +256,7 @@
         for gift in gifts:
             gift.start()
 
+    send(8 * core, 2, 0, 2, 0, same_half, (1,))
     for plane in range(2):
         send(2 - 2 * core, 8, plane, 1, 0, same_half, (1,))
 
@@ -340,6 +341,19 @@
         masks[0] = own_masks[:, :N]
         masks[1] = own_masks[:, N:]
 
+    def pass_list():
+        @pl.when(neg_slab != slab)
+        def _():
+            neg_copy.wait_recv()
+
+        @pl.when(core == 1)
+        def _():
+            neg_pass.start()
+
+    def neg_mask(slot, plane, at):
+        cells = neg_v[slot]
+        masks[at] = mask_of(cells, (lax.shift_right_logical(cells, 7) & 3) == plane, N, True)
+
     @pl.when(half == 1)
     def _():
         own_mask()
@@ -366,35 +380,29 @@
             (0, 1),
         )
         send(first_part, 4, 0, 2, 1 + pair, at_half, (0, 1))
-
-    @pl.when(neg_slab != slab)
-    def _():
-        neg_copy.wait_recv()
-
-    @pl.when(core == 1)
-    def _():
-        neg_pass.start()
+        if pair == 0:
+
+            @pl.when(half == 1)
+            def _():
+                pass_list()
+                neg_mask(core, 2 * core, 2)
 
     @pl.when(half == 0)
     def _():
+        pass_list()
         own_mask()
+        neg_mask(core, 2 * core, 2)
 
     own_row = pl.ds(pl.multiple_of(2 * owner, 2), 2)
     for part in range(PARTS):
         for plane in range(2):
             r_buf[part, plane, own_row, :] = y_buf[part, plane, own_row, :]
 
-    neg_cells = neg_v[core]
-    neg_plane = lax.shift_right_logical(neg_cells, 7) & 3
-    masks[2] = mask_of(neg_cells, neg_plane == 2 * core, N, True)
-
     @pl.when(core == 0)
     def _():
         neg_pass.wait_recv()
 
-    neg_cells = neg_v[1]
-    neg_plane = lax.shift_right_logical(neg_cells, 7) & 3
-    masks[3] = mask_of(neg_cells, neg_plane == 3 - 2 * core, N, True)
+    neg_mask(1, 3 - 2 * core, 3)
     loads[6].wait()
 
     def arrived(first_part, parts, chunk):

time: 51.5 us -> 51.3 us (level)
  no operation moved by 1% of the time
where the time goes in v5:
time: 51.3 us; the launch traced here: 51.2 us
  Pallas kernels  48.7 us (95%)
  local copies, waits for them, and re-layouts  1.81 us (4%)
  between operations  0.66 us (1%)
    pallas_call x1, Pallas kernels, per_device(): pl.pallas_call(kernel, out_shape=(jax.ShapeDtypeStruct((4, N), F32), jax....  48.7 us
    unnamed x6, local copies, waits for them, and re-layouts  1.81 us

profile of v5, /device:TPU:1, one launch (start us, length us, event | category | flops | bytes accessed | tf_op | source)
XLA Modules:
  0.0 51.2 jit_solution(3541896108177682744)
XLA Ops:
  0.6 0.0 copy-start
  0.6 0.0 copy-start.1
  0.7 0.6 %copy-done = f32[2]{0:T(128)S(1)} copy-done((f32[2]{0:T(128)S(1)}, f32[2]{0:T(128)}, u32[]{:S(2)}) %copy-start) | copy-done | bytes 32
  1.3 0.0 copy-done.1
  1.3 48.7 %shard_map.104 = (f32[4,128]{1,0:T(4,128)S(1)}, f32[3,3]{1,0:T(4,128)S(1)}) custom-call(f32[2,4,128,128]{3,2,1,0:T(8,128)} %orbitals.1, f32[2]{0:T(128)S(1)} %copy-done, s32[128,128]{1,0:T(8,128)} %bitcast.4, f32[3,512]{1,0:T(4,128)} %positions.1, s32[1,512]{1,0:T(1,128)} %bitcast.5, f32[4]{0:T(128)S(1)} %copy-done.1, ...), custom_call_target="tpu_custom_call" | custom-call | tf_op jit(solution)/shard_map/pallas_call | solution.py:583
  50.0 0.6 %copy.13 = f32[3,3]{1,0:T(4,128)} copy(f32[3,3]{1,0:T(4,128)S(1)} %get-tuple-element.8) | data formatting | bytes 72
  50.6 0.6 %copy.14 = f32[512]{0:T(512)} copy(f32[512]{0:T(512)S(1)} %bitcast.3) | data formatting | bytes 4096
Async XLA Ops:
  0.6 0.7 %copy-start = (f32[2]{0:T(128)S(1)}, f32[2]{0:T(128)}, u32[]{:S(2)}) copy-start(f32[2]{0:T(128)} %occupation_at.1) | copy-start | bytes 28
  0.6 0.7 %copy-start.1 = (f32[4]{0:T(128)S(1)}, f32[4]{0:T(128)}, u32[]{:S(2)}) copy-start(f32[4]{0:T(128)} %widths_at.1) | copy-start | bytes 52

commit v6 on v5

--- a/solution.py
+++ b/solution.py
@@ -122,7 +122,7 @@
             )
         )
     ]
-    for k in (7, 2, 4, 5, 3, 0, 1, 8, 6):
+    for k in (7, 2, 4, 5):
         loads[k].start()
     greet_bands = [[2 * (x // 2) + c for c in at_core] for x in at_x]
     greet_slabs = [[4 * lax.rem(x, 2) + y for y in at_y] for x in at_x]
@@ -130,6 +130,9 @@
         pl.semaphore_signal(
             barrier, 1, **device(greet_bands[dx][dc], greet_slabs[dx][dy] + at_z[dz])
         )
+
+    for k in (3, 0, 1, 8, 6):
+        loads[k].start()
 
     loads[7].wait()
     loads[2].wait()
@@ -627,18 +630,23 @@
             dma((4,)),
         ],
         compiler_params=pltpu.CompilerParams(
-            collective_id=0, has_side_effects=True, vmem_limit_bytes=56538000
+            collective_id=0, has_side_effects=True, vmem_limit_bytes=48 << 20
         ),
     )(
-        orbitals,
-        occupation,
-        g_list.reshape(N, N),
-        positions,
-        species.reshape(1, ATOMS),
-        widths,
-        jnp.asarray(right_table),
-        jnp.asarray(left_table),
-        jnp.asarray(x_table),
+        *(
+            pltpu.with_memory_space_constraint(operand, pltpu.HBM)
+            for operand in (
+                orbitals,
+                occupation,
+                g_list.reshape(N, N),
+                positions,
+                species.reshape(1, ATOMS),
+                widths,
+                jnp.asarray(right_table),
+                jnp.asarray(left_table),
+                jnp.asarray(x_table),
+            )
+        )
     )
     return stress, atoms.reshape(ATOMS)
 

time: 51.3 us -> 50.8 us (level)
  local copies, waits for them, and re-layouts: 1.81 us -> 1.16 us
    unnamed x6 -> x2, local copies, waits for them, and re-layouts: 1.81 us -> 1.16 us
where the time goes in v6:
time: 50.8 us; the launch traced here: 50.7 us
  Pallas kernels  48.9 us (96%)
  local copies, waits for them, and re-layouts  1.16 us (2%)
  between operations  0.64 us (1%)
    pallas_call x1, Pallas kernels, per_device(): pl.pallas_call(kernel, out_shape=(jax.ShapeDtypeStruct((4, N), F32), jax....  48.9 us
    unnamed x2, local copies, waits for them, and re-layouts  1.16 us

profile of v6, /device:TPU:1, one launch (start us, length us, event | category | flops | bytes accessed | tf_op | source)
XLA Modules:
  0.0 50.7 jit_solution(1798976294357792361)
XLA Ops:
  0.6 48.9 %shard_map.104 = (f32[4,128]{1,0:T(4,128)S(1)}, f32[3,3]{1,0:T(4,128)S(1)}) custom-call(f32[2,4,128,128]{3,2,1,0:T(8,128)} %orbitals.1, f32[2]{0:T(128)} %occupation_at.1, s32[128,128]{1,0:T(8,128)} %bitcast.4, f32[3,512]{1,0:T(4,128)} %positions.1, s32[1,512]{1,0:T(1,128)} %bitcast.5, f32[4]{0:T(128)} %widths_at.1, ...), custom_call_target="tpu_custom_call" | custom-call | tf_op jit(solution)/shard_map/pallas_call | solution.py:586
  49.5 0.6 %copy.13 = f32[3,3]{1,0:T(4,128)} copy(f32[3,3]{1,0:T(4,128)S(1)} %get-tuple-element.8) | data formatting | bytes 72
  50.1 0.6 %copy.14 = f32[512]{0:T(512)} copy(f32[512]{0:T(512)S(1)} %bitcast.3) | data formatting | bytes 4096

commit v7 on v6

--- a/solution.py
+++ b/solution.py
@@ -80,7 +80,7 @@
     orbitals, occupation_at, g_list, positions, species, widths_at, right_table, left_table, x_table,
     out_atoms, out_stress,
     occupation, widths, orb_v, list_v, neg_v, pos_v, spec_v, right_v, left_v, tx_v,
-    psi, y_buf, r_buf, z_re, z_im, zc_re, zc_im, x_re, x_im, col_x, col_z, masks, coefs,
+    psi, y_buf, r_buf, z_re, z_im, zc_re, zc_im, x_re, x_im, x_flip, col_x, col_z, masks, coefs,
     red_src, red_x, red_mid, red_yz,
     load_sem, mate_sem, cross_send, cross_recv, neg_sem, pass_sem, a2a_send, a2a_recv, red_sem,
 ):
@@ -202,6 +202,18 @@
 
     pl.semaphore_wait(barrier, len(GREETED))
 
+    def trade(to_band, to_core, send_sem, recv_sem):
+        return pltpu.make_async_remote_copy(
+            orb_v.at[:, pl.ds(2 * to_core, 2)],
+            psi.at[pl.ds(2 * band, 2)],
+            send_sem,
+            recv_sem,
+            **device(to_band, slab),
+        )
+
+    mate_trade = trade(mate, 1 - core, mate_sem.at[0], mate_sem.at[1])
+    mate_trade.start()
+
     loads[3].wait()
     neg_slab = jnp.where(core == 0, lax.rem(32 - slab, 32), 31 - slab)
     neg_copy = pltpu.make_async_remote_copy(
@@ -219,15 +231,6 @@
     def _():
         neg_v[core] = list_v[...]
 
-    def trade(to_band, to_core, send_sem, recv_sem):
-        return pltpu.make_async_remote_copy(
-            orb_v.at[:, pl.ds(2 * to_core, 2)],
-            psi.at[pl.ds(2 * band, 2)],
-            send_sem,
-            recv_sem,
-            **device(to_band, slab),
-        )
-
     gives = jnp.logical_or(half == 0, core == low)
     gives_late = jnp.logical_and(half == 0, core == 1)
     gifts = [
@@ -240,8 +243,6 @@
         for gift in gifts:
             gift.start()
 
-    mate_trade = trade(mate, 1 - core, mate_sem.at[0], mate_sem.at[1])
-    mate_trade.start()
     send(8 * core, 2, 0, 2, 0, same_half, (0,))
 
     mate_trade.wait_recv()
@@ -438,6 +439,8 @@
             totals[k] = term if totals[k] is None else totals[k] + term
         return totals
 
+    x_flip[...] = jnp.where(iota((N, ATOMS), 0) == N // 2, -x_im[...], x_im[...])
+
     cell_x = iota((N, N), 0)
     cell_z = iota((N, N), 1)
     wave_x = (TWO_PI / N) * fold(cell_x).astype(F32)
@@ -504,8 +507,7 @@
 
     proj_re = projected(rows_re, zc_re)
     proj_im = projected(rows_im, zc_im)
-    ex_re, ex_im = x_re[...], x_im[...]
-    flip_im = jnp.where(iota((N, ATOMS), 0) == N // 2, -ex_im, ex_im)
+    ex_re, ex_im, flip_im = x_re[...], x_im[...], x_flip[...]
     atoms = jnp.zeros((1, ATOMS), F32)
     for n in range(4):
         re_part = proj_re[n * N : (n + 1) * N]
@@ -609,6 +611,7 @@
             pltpu.VMEM((N, ATOMS), F32),
             pltpu.VMEM((3 * N, ATOMS), BF16),
             pltpu.VMEM((3 * N, ATOMS), BF16),
+            pltpu.VMEM((N, ATOMS), F32),
             pltpu.VMEM((N, ATOMS), F32),
             pltpu.VMEM((N, ATOMS), F32),
             pltpu.VMEM((N, N), F32),

time: 50.8 us -> 50.8 us (level)
  no operation moved by 1% of the time
where the time goes in v7:
time: 50.8 us; the launch traced here: 50.7 us
  Pallas kernels  48.9 us (96%)
  local copies, waits for them, and re-layouts  1.16 us (2%)
  between operations  0.64 us (1%)
    pallas_call x1, Pallas kernels, per_device(): pl.pallas_call(kernel, out_shape=(jax.ShapeDtypeStruct((4, N), F32), jax....  48.9 us
    unnamed x2, local copies, waits for them, and re-layouts  1.16 us

profile of v7, /device:TPU:1, one launch (start us, length us, event | category | flops | bytes accessed | tf_op | source)
XLA Modules:
  0.0 50.7 jit_solution(2022869525081508697)
XLA Ops:
  0.6 48.9 %shard_map.104 = (f32[4,128]{1,0:T(4,128)S(1)}, f32[3,3]{1,0:T(4,128)S(1)}) custom-call(f32[2,4,128,128]{3,2,1,0:T(8,128)} %orbitals.1, f32[2]{0:T(128)} %occupation_at.1, s32[128,128]{1,0:T(8,128)} %bitcast.4, f32[3,512]{1,0:T(4,128)} %positions.1, s32[1,512]{1,0:T(1,128)} %bitcast.5, f32[4]{0:T(128)} %widths_at.1, ...), custom_call_target="tpu_custom_call" | custom-call | tf_op jit(solution)/shard_map/pallas_call | solution.py:588
  49.5 0.6 %copy.13 = f32[3,3]{1,0:T(4,128)} copy(f32[3,3]{1,0:T(4,128)S(1)} %get-tuple-element.8) | data formatting | bytes 72
  50.1 0.6 %copy.14 = f32[512]{0:T(512)} copy(f32[512]{0:T(512)S(1)} %bitcast.3) | data formatting | bytes 4096

commit v8 on v7

--- a/solution.py
+++ b/solution.py
@@ -122,8 +122,6 @@
             )
         )
     ]
-    for k in (7, 2, 4, 5):
-        loads[k].start()
     greet_bands = [[2 * (x // 2) + c for c in at_core] for x in at_x]
     greet_slabs = [[4 * lax.rem(x, 2) + y for y in at_y] for x in at_x]
     for dx, dy, dz, dc in GREETED:
@@ -131,7 +129,7 @@
             barrier, 1, **device(greet_bands[dx][dc], greet_slabs[dx][dy] + at_z[dz])
         )
 
-    for k in (3, 0, 1, 8, 6):
+    for k in (7, 2, 4, 5, 3, 0, 1, 8, 6):
         loads[k].start()
 
     loads[7].wait()

time: 50.8 us -> 50.8 us (level)
  no operation moved by 1% of the time
where the time goes in v8:
time: 50.8 us; the launch traced here: 50.7 us
  Pallas kernels  48.9 us (96%)
  local copies, waits for them, and re-layouts  1.16 us (2%)
  between operations  0.64 us (1%)
    pallas_call x1, Pallas kernels, per_device(): pl.pallas_call(kernel, out_shape=(jax.ShapeDtypeStruct((4, N), F32), jax....  48.9 us
    unnamed x2, local copies, waits for them, and re-layouts  1.16 us

profile of v8, /device:TPU:1, one launch (start us, length us, event | category | flops | bytes accessed | tf_op | source)
XLA Modules:
  0.0 50.7 jit_solution(6163971517055428871)
XLA Ops:
  0.6 48.9 %shard_map.104 = (f32[4,128]{1,0:T(4,128)S(1)}, f32[3,3]{1,0:T(4,128)S(1)}) custom-call(f32[2,4,128,128]{3,2,1,0:T(8,128)} %orbitals.1, f32[2]{0:T(128)} %occupation_at.1, s32[128,128]{1,0:T(8,128)} %bitcast.4, f32[3,512]{1,0:T(4,128)} %positions.1, s32[1,512]{1,0:T(1,128)} %bitcast.5, f32[4]{0:T(128)} %widths_at.1, ...), custom_call_target="tpu_custom_call" | custom-call | tf_op jit(solution)/shard_map/pallas_call | solution.py:586
  49.5 0.6 %copy.13 = f32[3,3]{1,0:T(4,128)} copy(f32[3,3]{1,0:T(4,128)S(1)} %get-tuple-element.8) | data formatting | bytes 72
  50.1 0.6 %copy.14 = f32[512]{0:T(512)} copy(f32[512]{0:T(512)S(1)} %bitcast.3) | data formatting | bytes 4096
